TPU v7x, 32 devices: a whole 2x2x4 slice. The times are simulated.
32 devices in a mesh: ctx: 16 (over z, x, core), head: 2 (over y).
Axes of the slice: x: 2, y: 2, z: 4, core: 2. Of those that a mesh axis runs over, the one named last changes fastest.
Arguments:
- tokens: bfloat16 [4096, 4096], P('ctx', 'head'), may hold values from -19.8 to 19.8
- query_weight: bfloat16 [4096, 4096], P('ctx', 'head'), may hold values from -0.09375 to 0.09375
- key_weight: bfloat16 [4096, 4096], P('ctx', 'head'), may hold values from -0.09375 to 0.09375
- value_weight: bfloat16 [4096, 4096], P('ctx', 'head'), may hold values from -0.09375 to 0.09375
- output_weight: bfloat16 [4096, 4096], P('ctx', 'head'), may hold values from -0.29882812 to 0.29882812
- adapter_down: bfloat16 [3, 8, 4096], replicated, may hold values from -0.09375 to 0.09375
- adapter_up: bfloat16 [3, 8, 4096], P(None, None, 'head'), may hold values from -0.8984375 to 0.8984375
Outputs:
- attended: bfloat16 [4096, 4096], P('ctx', 'head')
All inputs are finite; a program needn't handle non-finite values.
Results may differ from a plain program's by a relative error of at most 0.012.
Values may be sent and summed in bfloat16 or wider, within the bound.
No kernel may reach another device: no remote copies, remote signals or barrier semaphores. Data moves between devices by JAX's collectives and lax.ppermute only.
A program may use at most 128 MiB of HBM per device.

v0:
```python
import functools

import jax
import jax.numpy as jnp
from jax import lax
from jax.experimental import pallas as pl
from jax.experimental.pallas import tpu as pltpu
from jax.sharding import PartitionSpec as P

D = 4096
HEADS = 32
GROUP_DEV = 16


def shifted(x, axis, by):
    peers = lax.axis_size(axis)
    return lax.ppermute(x, axis, [(i, (i + by) % peers) for i in range(peers)])


def rotary(projection, positions):
    half_dim = projection.shape[-1] // 2
    inverse_freq = 10000.0 ** (
        -(jnp.arange(half_dim, dtype=jnp.float32) * 2.0) / projection.shape[-1]
    )
    angles = positions.astype(jnp.float32)[:, None] * inverse_freq[None, :]
    cosine = jnp.cos(angles)[:, None, :]
    sine_part = jnp.sin(angles)[:, None, :]
    first_half = projection[..., :half_dim]
    second = projection[..., half_dim:]
    return jnp.concatenate(
        [first_half * cosine - second * sine_part, second * cosine + first_half * sine_part], -1
    )


def fold_rows(left_side, weight_piece):
    return jnp.dot(left_side, weight_piece, preferred_element_type=jnp.float32)


def update_block(carry, query, key_blk, value_blk, key_place, query_pos, group_size):
    row_max, denominator, running = carry
    scale = query.shape[-1] ** (-0.5)
    scores = jnp.einsum("qhd,khd->hqk", query, key_blk, preferred_element_type=jnp.float32) * scale
    allowed = ((query_pos // group_size)[:, None] == (key_place // group_size)[None, :]) & (
        key_place[None, :] <= query_pos[:, None]
    )
    scores = jnp.where(allowed[None], scores, -1e30)
    new_max = jnp.maximum(row_max, jnp.max(scores, axis=-1))
    weights = jnp.where(allowed[None], jnp.exp(scores - new_max[..., None]), 0.0)
    factor = jnp.exp(row_max - new_max)
    denominator = denominator * factor + jnp.sum(weights, axis=-1)
    running = running * factor[..., None] + jnp.einsum(
        "hqk,khd->hqd", weights.astype(jnp.bfloat16), value_blk, preferred_element_type=jnp.float32
    )
    return (new_max, denominator, running)


def per_device(
    tokens, query_weight, key_weight, value_weight, output_weight, adapter_down, adapter_up
):
    tok_rows = tokens.shape[0]
    ctx_count = lax.axis_size("ctx")
    ctx_index = lax.axis_index("ctx")
    head_count = lax.axis_size("head")
    heads_dev = HEADS // head_count
    head_dim = D // HEADS
    slab_len = tok_rows * ctx_count
    group_size = GROUP_DEV * tok_rows
    shift_span = group_size // 2
    shifted_dev = lax.axis_index("head") >= head_count // 2
    features = lax.all_gather(tokens, "head", axis=1, tiled=True)

    def fold_one(weight_piece):
        return fold_rows(features, weight_piece)

    projected = (
        fold_one(lax.all_gather(query_weight, "ctx", axis=0, tiled=True)),
        fold_one(lax.all_gather(key_weight, "ctx", axis=0, tiled=True)),
        fold_one(lax.all_gather(value_weight, "ctx", axis=0, tiled=True)),
    )
    low_ranks = jnp.einsum(
        "td,jrd->jtr", features, adapter_down, preferred_element_type=jnp.float32
    ).astype(jnp.bfloat16)
    local_rows = jnp.arange(tok_rows, dtype=jnp.int32)
    positions = ctx_index * tok_rows + local_rows
    full_projs = []
    for which in range(3):
        full_proj = projected[which] + 2.0 * jnp.dot(
            low_ranks[which], adapter_up[which], preferred_element_type=jnp.float32
        )
        full_projs.append(full_proj.reshape(tok_rows, heads_dev, head_dim))
    query = rotary(full_projs[0], positions).astype(jnp.bfloat16)
    key_rot = rotary(full_projs[1], positions).astype(jnp.bfloat16)
    value = full_projs[2].astype(jnp.bfloat16)
    key_value = jnp.stack([key_rot, value])
    offset = jnp.where(shifted_dev, shift_span, 0).astype(jnp.int32)
    query_pos = (positions - offset) % slab_len
    start_carry = (
        jnp.full((heads_dev, tok_rows), -1e30, jnp.float32),
        jnp.zeros((heads_dev, tok_rows), jnp.float32),
        jnp.zeros((heads_dev, tok_rows, head_dim), jnp.float32),
    )
    carry = update_block(start_carry, query, key_rot, value, query_pos, query_pos, group_size)

    def one_turn(turn, state):
        current, running_carry = state
        current = shifted(current, "ctx", 1)
        source = (ctx_index - turn - 1) % ctx_count
        key_place = (source * tok_rows + local_rows - offset) % slab_len
        running_carry = update_block(
            running_carry, query, current[0], current[1], key_place, query_pos, group_size
        )
        return (current, running_carry)

    _, carry = lax.fori_loop(0, GROUP_DEV - 1, one_turn, (key_value, carry))
    _, denominator, running = carry
    result = (running / denominator[..., None]).astype(jnp.bfloat16)
    result = result.transpose(1, 0, 2).reshape(tok_rows, heads_dev * head_dim)
    merged = lax.all_gather(result, "head", axis=1, tiled=True)
    attended = fold_rows(merged, lax.all_gather(output_weight, "ctx", axis=0, tiled=True))
    return attended.astype(jnp.bfloat16)


def exchanged(x, axis, bit):
    peers = lax.axis_size(axis)
    return lax.ppermute(x, axis, [(i, i ^ bit) for i in range(peers)])


def sent(x, pairs):
    return lax.ppermute(x, "ctx", pairs)


def line_gather(own, plane):
    z_index = lax.axis_index("ctx") // plane

    def hops(steps):
        return [(a * plane + i, b * plane + i) for a, b in steps for i in range(plane)]

    inner = (z_index == 1) | (z_index == 2)
    middle = hops([(1, 2), (2, 1)])
    outward = hops([(1, 0), (2, 3)])
    near = sent(own, hops([(0, 1), (1, 0), (2, 3), (3, 2)]))
    first = sent(own, middle)
    first_out = sent(first, outward)
    far = sent(near, middle)
    far_out = sent(far, outward)
    return [own, near, jnp.where(inner, first, first_out), jnp.where(inner, far, far_out)]


def line_sources(z_index):
    low = z_index < 2
    return [z_index, z_index ^ 1, jnp.where(low, 2, 1), jnp.where(low, 3, 0)]


def flash_kernel(table, *refs, head_dim, block, piece):
    *parts, out, query, key, value = refs
    own, peer = parts[: len(parts) // 2], parts[len(parts) // 2 :]
    slab_len = query.shape[0]
    entry = 0
    for pair in zip(own, peer):
        for part in range(pair[0].shape[0] // piece):
            rows = slice(part * piece, (part + 1) * piece)
            for source in pair:
                place = pl.ds(pl.multiple_of(table[entry] * piece, piece), piece)
                query[place, :] = source[rows, :head_dim]
                key[place, :] = source[rows, head_dim : 2 * head_dim]
                value[place, :] = source[rows, 2 * head_dim :]
                entry += 1
    offset = table[entry]
    scale = head_dim ** (-0.5) * 1.4426950408889634
    diagonal = lax.broadcasted_iota(jnp.int32, (block, block), 1) <= lax.broadcasted_iota(
        jnp.int32, (block, block), 0
    )
    contract = (((1,), (1,)), ((), ()))
    for step in range(slab_len // block):
        rows = slice(step * block, (step + 1) * block)
        q_blk = query[rows, :]
        corner = lax.dot_general(q_blk, key[rows, :], contract, preferred_element_type=jnp.float32)
        corner = jnp.where(diagonal, corner, -1e30)
        top = jnp.max(corner, axis=-1, keepdims=True)
        if step:
            before = lax.dot_general(
                q_blk, key[: step * block, :], contract, preferred_element_type=jnp.float32
            )
            top = jnp.maximum(top, jnp.max(before, axis=-1, keepdims=True))
        weights = jnp.exp2((corner - top) * scale)
        total = jnp.sum(weights, axis=-1, keepdims=True)
        mixed = jnp.dot(
            weights.astype(jnp.bfloat16), value[rows, :], preferred_element_type=jnp.float32
        )
        if step:
            weights = jnp.exp2((before - top) * scale)
            total += jnp.sum(weights, axis=-1, keepdims=True)
            mixed += jnp.dot(
                weights.astype(jnp.bfloat16),
                value[: step * block, :],
                preferred_element_type=jnp.float32,
            )
        start = lax.rem(offset + step * block, slab_len)
        out[pl.ds(pl.multiple_of(start, block), block), :] = (mixed / total).astype(jnp.bfloat16)


def flash(table, own, peer, slab_len, head_dim, piece, block=256):
    body = functools.partial(flash_kernel, head_dim=head_dim, block=block, piece=piece)
    vmem = pl.BlockSpec(memory_space=pltpu.VMEM)
    scratch = [pltpu.VMEM((slab_len, head_dim), jnp.bfloat16)] * 3
    return pl.pallas_call(
        body,
        out_shape=jax.ShapeDtypeStruct((slab_len, head_dim), jnp.bfloat16),
        in_specs=[pl.BlockSpec(memory_space=pltpu.SMEM)] + [vmem] * (2 * len(own)),
        out_specs=vmem,
        scratch_shapes=scratch,
        compiler_params=pltpu.CompilerParams(vmem_limit_bytes=48 * 2**20),
        name="flash",
    )(table, *own, *peer)


def project_kernel(*refs, head_dim):
    *inputs, down, up, cosine, sine, mine, other, total = refs
    pieces, weights = inputs[:-6], inputs[-6:]
    step = pl.program_id(0)
    rows = jnp.concatenate([piece[...] for piece in pieces], 0)

    @pl.when(step == 0)
    def _():
        total[...] = jnp.zeros_like(total)

    wide = 2 * head_dim
    for which in range(3):
        pair = jnp.concatenate([weights[which][...], weights[which + 3][...]], 1)
        total[:, which * wide : (which + 1) * wide] += fold_rows(rows, pair)
    total[:, 3 * wide :] += fold_rows(rows, down[...])

    @pl.when(step == pl.num_programs(0) - 1)
    def _():
        low = total[:, 3 * wide :].astype(jnp.bfloat16)
        for which in range(3):
            for side, out in enumerate((mine, other)):
                start = which * wide + side * head_dim
                proj = total[:, start : start + head_dim] + 2.0 * fold_rows(
                    low, up[:, start : start + head_dim]
                )
                if which < 2:
                    turned = pltpu.roll(proj, head_dim // 2, 1)
                    proj = proj * cosine[...] + turned * sine[...]
                out[:, which * head_dim : (which + 1) * head_dim] = proj.astype(jnp.bfloat16)


def project(pieces, weights, down, up, cosine, sine, head_dim, depth=1024):
    rows = sum(piece.shape[0] for piece in pieces)
    width = weights[0].shape[0]
    whole = lambda shape: pl.BlockSpec(shape, lambda k: (0, 0))
    out = jax.ShapeDtypeStruct((rows, 3 * head_dim), jnp.bfloat16)
    return pl.pallas_call(
        functools.partial(project_kernel, head_dim=head_dim),
        grid=(width // depth,),
        out_shape=(out, out),
        in_specs=[pl.BlockSpec((piece.shape[0], depth), lambda k: (0, k)) for piece in pieces]
        + [pl.BlockSpec((depth, head_dim), lambda k: (k, 0))] * 6
        + [pl.BlockSpec((depth, down.shape[1]), lambda k: (k, 0))]
        + [whole(up.shape), whole(cosine.shape), whole(sine.shape)],
        out_specs=[whole(out.shape)] * 2,
        scratch_shapes=[pltpu.VMEM((rows, 6 * head_dim + down.shape[1]), jnp.float32)],
        compiler_params=pltpu.CompilerParams(vmem_limit_bytes=40 * 2**20),
        name="project",
    )(*pieces, *weights, down, up, cosine, sine)


def output_kernel(table, *refs):
    *pieces, mine, other, out, heads, left = refs
    count, _, head_dim = mine.shape

    @pl.when(pl.program_id(0) == 0)
    def _():
        first = table[len(pieces)]
        heads[pl.ds(first, count)] = mine[...]
        heads[pl.ds(count - first, count)] = other[...]
        for at in range(2 * count):
            piece, inner = divmod(at * head_dim, pieces[0].shape[0])
            head = table[piece] * (pieces[0].shape[0] // head_dim) + inner // head_dim
            left[:, at * head_dim : (at + 1) * head_dim] = heads[head]

    weight = jnp.concatenate([piece[...] for piece in pieces], 0)
    out[...] = fold_rows(left[...], weight).astype(jnp.bfloat16)


def output_project(table, pieces, mine, other, wide=256):
    count, rows, head_dim = mine.shape
    cols = pieces[0].shape[1]
    part = pl.BlockSpec((pieces[0].shape[0], wide), lambda n: (0, n))
    whole = pl.BlockSpec(mine.shape, lambda n: (0, 0, 0))
    return pl.pallas_call(
        output_kernel,
        grid=(cols // wide,),
        out_shape=jax.ShapeDtypeStruct((rows, cols), jnp.bfloat16),
        in_specs=[pl.BlockSpec(memory_space=pltpu.SMEM)] + [part] * len(pieces) + [whole] * 2,
        out_specs=pl.BlockSpec((rows, wide), lambda n: (0, n)),
        scratch_shapes=[
            pltpu.VMEM((2 * count, rows, head_dim), jnp.bfloat16),
            pltpu.VMEM((rows, 2 * count * head_dim), jnp.bfloat16),
        ],
        compiler_params=pltpu.CompilerParams(vmem_limit_bytes=40 * 2**20),
        name="output",
    )(table, *pieces, mine, other)


def one_head_per_device(*args):
    return attention_layer(*args)


def attention_layer(
    tokens, query_weight, key_weight, value_weight, output_weight, adapter_down, adapter_up
):
    tok_rows = tokens.shape[0]
    ctx_count = lax.axis_size("ctx")
    ctx_index = lax.axis_index("ctx")
    y_index = lax.axis_index("head")
    head_dim = D // HEADS
    slab_len = tok_rows * ctx_count
    plane = ctx_count // 4
    half = tok_rows // 2
    z_index, in_plane = ctx_index // plane, ctx_index % plane
    rank = adapter_down.shape[1]

    kept = lax.dynamic_slice_in_dim(tokens, y_index * half, half, 0)
    other = lax.dynamic_slice_in_dim(tokens, (1 - y_index) * half, half, 0)
    came = exchanged(other, "head", 1)
    shard = jnp.where(
        y_index == 0, jnp.concatenate([kept, came], 1), jnp.concatenate([came, kept], 1)
    )

    def spread(own):
        line = line_gather(own, plane)
        groups = []
        for piece in line:
            across = exchanged(piece, "ctx", 2)
            beside = exchanged(piece, "ctx", 1)
            groups.append([piece, beside, across, exchanged(across, "ctx", 1)])
        return groups

    slots = spread(shard)

    def swap(weight):
        return lax.all_to_all(weight, "ctx", split_axis=1, concat_axis=0, tiled=True)

    mine = [swap(weight) for weight in (query_weight, key_weight, value_weight)]
    pair_weights = mine + [exchanged(weight, "head", 1) for weight in mine]

    down = jnp.pad(adapter_down.reshape(3 * rank, D).T, ((0, 0), (0, head_dim - 3 * rank)))
    up_mine = lax.dynamic_slice_in_dim(adapter_up, ctx_index * head_dim, head_dim, 2)
    up_pair = jnp.concatenate([up_mine, exchanged(up_mine, "head", 1)], 2)
    up = jnp.zeros((head_dim, 6 * head_dim), jnp.bfloat16)
    for which in range(3):
        up = lax.dynamic_update_slice(up, up_pair[which], (which * rank, which * 2 * head_dim))

    variant = jnp.array([0, 1, 2, 3], dtype=jnp.int32)
    local = jnp.arange(half, dtype=jnp.int32)
    inverse_freq = 10000.0 ** (-(jnp.arange(head_dim // 2, dtype=jnp.float32) * 2.0) / head_dim)
    places = [z * plane + (in_plane ^ variant) for z in line_sources(z_index)]
    own_parts, peer_parts = [], []
    for first, last in GROUPS:
        rows_from = jnp.concatenate(places[first:last])[:, None] * tok_rows
        positions = (rows_from + y_index * half + local[None, :]).reshape(-1)
        angles = positions.astype(jnp.float32)[:, None] * inverse_freq[None, :]
        cosine, sine = jnp.cos(angles), jnp.sin(angles)
        cosine = jnp.concatenate([cosine, cosine], 1)
        sine = jnp.concatenate([-sine, sine], 1)
        pieces = [piece for slot in slots[first:last] for piece in slot]
        own_part, peer_part = project(pieces, pair_weights, down, up, cosine, sine, head_dim)
        own_parts.append(own_part)
        peer_parts.append(exchanged(peer_part, "head", 1))

    sources = jnp.concatenate(places)
    shift = jnp.where(y_index * ctx_count + ctx_index >= HEADS // 2, slab_len // 2, 0)
    sides = jnp.stack([y_index, 1 - y_index]).astype(jnp.int32)
    table = (sources[:, None] * 2 + sides[None, :]).reshape(-1)
    table = (table - shift // half) % (slab_len // half)
    table = jnp.concatenate([table, shift[None]]).astype(jnp.int32)
    result = flash(table, own_parts, peer_parts, slab_len, head_dim, half)
    blocks = result.reshape(ctx_count, tok_rows, head_dim)
    mixed = lax.all_to_all(blocks, "ctx", split_axis=0, concat_axis=0, tiled=True)
    mixed_other = exchanged(mixed, "head", 1)

    pieces = [piece for group in spread(output_weight) for piece in group]
    heads_first = y_index * ctx_count
    out_table = jnp.concatenate([sources, heads_first[None]]).astype(jnp.int32)
    return output_project(out_table, pieces, mixed, mixed_other)


GROUPS = ((0, 3), (3, 4))


def one_head_fits(mesh):
    ctx_count, head_count = mesh.shape["ctx"], mesh.shape["head"]
    return ctx_count == GROUP_DEV and ctx_count // 4 == 4 and HEADS == ctx_count * head_count and head_count == 2


def solution(mesh):
    fits = one_head_fits(mesh)
    body = one_head_per_device if fits else per_device
    in_specs = (
        P("ctx", "head"),
        P("ctx", "head"),
        P("ctx", "head"),
        P("ctx", "head"),
        P("ctx", "head"),
        P(),
        P(None, None, "head"),
    )
    out_specs = P("ctx", "head")
    return jax.shard_map(
        body, mesh=mesh, in_specs=in_specs, out_specs=out_specs, check_vma=False
    )
```

profile of v0, /device:TPU:0, one launch (start us, length us, event | category | flops | bytes accessed | tf_op | source)
XLA Modules:
  0.0 414.3 jit_solution(13828431516379799435)
XLA Ops:
  2.5 7.4 %all-to-all-start = ((bf16[256,16,128]{2,0,1:T(8,128)(2,1)}), bf16[256,16,128]{2,0,1:T(8,128)(2,1)S(1)}, u32[]{:S(2)}, u32[]{:S(2)}) async-start(bf16[256,16,128]{2,0,1:T(8,128)(2,1)} %copy_bitcast_fusion.2), calls=%async_computation | async-start | bytes 2097152 | tf_op jit(solution)/shard_map/all_to_all | solution.py:343
  9.9 2.2 constant_dynamic-slice_fusion.2
  14.8 17.9 %all-to-all-done = bf16[256,16,128]{2,0,1:T(8,128)(2,1)S(1)} async-done(((bf16[256,16,128]{2,0,1:T(8,128)(2,1)}), bf16[256,16,128]{2,0,1:T(8,128)(2,1)S(1)}, u32[]{:S(2)}, u32[]{:S(2)}) %all-to-all-start) | async-done | bytes 1048608 | tf_op jit(solution)/shard_map/all_to_all | solution.py:343
  32.8 6.8 %all-to-all-start.1 = ((bf16[256,16,128]{2,0,1:T(8,128)(2,1)}), bf16[256,16,128]{2,0,1:T(8,128)(2,1)S(1)}, u32[]{:S(2)}, u32[]{:S(2)}) async-start(bf16[256,16,128]{2,0,1:T(8,128)(2,1)} %copy_bitcast_fusion.1), calls=%async_computation.1 | async-start | bytes 2097152 | tf_op jit(solution)/shard_map/all_to_all | solution.py:343
  40.8 1.9 collective-permute-start.21
  44.4 3.3 collective-permute-start.3
  49.1 33.6 %collective-permute-done.21.refs_4_ = bf16[128,4096]{1,0:T(8,128)(2,1)} collective-permute-done((bf16[128,4096]{1,0:T(8,128)(2,1)}, bf16[128,4096]{1,0:T(8,128)(2,1)}, u32[]{:S(2)}, u32[]{:S(2)}) %collective-permute-start.21) | collective-permute-done | bytes 1048608 | tf_op jit(solution)/shard_map/ppermute | solution.py:129
  82.6 1.7 collective-permute-start.34
  86.9 8.7 %all-to-all-start.2 = ((bf16[256,16,128]{2,0,1:T(8,128)(2,1)}), bf16[256,16,128]{2,0,1:T(8,128)(2,1)S(1)}, u32[]{:S(2)}, u32[]{:S(2)}) async-start(bf16[256,16,128]{2,0,1:T(8,128)(2,1)} %copy_bitcast_fusion), calls=%async_computation.2 | async-start | bytes 2097152 | tf_op jit(solution)/shard_map/all_to_all | solution.py:343
  97.9 2.0 collective-permute-done.33
  99.9 5.2 %collective-permute-done.3.refs_4_ = bf16[256,2048]{1,0:T(8,128)(2,1)} collective-permute-done((bf16[256,2048]{1,0:T(8,128)(2,1)}, bf16[256,2048]{1,0:T(8,128)(2,1)}, u32[]{:S(2)}, u32[]{:S(2)}) %collective-permute-start.3) | collective-permute-done | bytes 1048608 | tf_op jit(solution)/shard_map/ppermute | solution.py:129
  107.2 31.6 %collective-permute-done.26 = bf16[128,4096]{1,0:T(8,128)(2,1)} collective-permute-done((bf16[128,4096]{1,0:T(8,128)(2,1)}, bf16[128,4096]{1,0:T(8,128)(2,1)}, u32[]{:S(2)}, u32[]{:S(2)}) %collective-permute-start.26) | collective-permute-done | bytes 1048608 | tf_op jit(solution)/shard_map/ppermute | solution.py:129
  140.1 2.3 broadcast_select_fusion.1.refs_8_
  147.6 18.8 %collective-permute-done.35 = bf16[128,4096]{1,0:T(8,128)(2,1)} collective-permute-done((bf16[128,4096]{1,0:T(8,128)(2,1)}, bf16[128,4096]{1,0:T(8,128)(2,1)}, u32[]{:S(2)}, u32[]{:S(2)}) %collective-permute-start.35) | collective-permute-done | bytes 1048608 | tf_op jit(solution)/shard_map/ppermute | solution.py:129
  166.3 2.3 broadcast_select_fusion.refs_0_
  169.3 21.8 %collective-permute-done.31.refs_16_.refs_8_ = bf16[4096,128]{1,0:T(8,128)(2,1)} collective-permute-done((bf16[4096,128]{1,0:T(8,128)(2,1)S(1)}, bf16[4096,128]{1,0:T(8,128)(2,1)}, u32[]{:S(2)}, u32[]{:S(2)}) %collective-permute-start.31) | collective-permute-done | bytes 1048608 | tf_op jit(solution)/shard_map/ppermute | solution.py:125
  192.5 4.5 %fusion = (f32[1536,64]{1,0:T(8,128)}, f32[1536,64]{1,0:T(8,128)}, f32[1536,64]{1,0:T(8,128)}) fusion(f32[64]{0:T(128)S(1)} %multiply_power_fusion, f32[1536]{0:T(1024)S(1)} %convert_bitcast_fusion), kind=kLoop, calls=%fused_computation.16 | loop fusion | flops 196608 | bytes 1186048 | tf_op jit(solution)/shard_map/neg | solution.py:366
  198.4 2.5 pad.5.refs_18_.refs_10_
  200.9 10.7 %collective-permute-done.32.refs_17_.refs_9_ = bf16[4096,128]{1,0:T(8,128)(2,1)} collective-permute-done((bf16[4096,128]{1,0:T(8,128)(2,1)S(1)}, bf16[4096,128]{1,0:T(8,128)(2,1)}, u32[]{:S(2)}, u32[]{:S(2)}) %collective-permute-start.32) | collective-permute-done | bytes 1048608 | tf_op jit(solution)/shard_map/ppermute | solution.py:125
  211.5 1.7 collective-permute-start.7
  213.3 1.7 collective-permute-start.12
  218.4 20.2 %project.2 = (bf16[1536,384]{1,0:T(8,128)(2,1)}, bf16[1536,384]{1,0:T(8,128)(2,1)}) custom-call(bf16[128,4096]{1,0:T(8,128)(2,1)} %maximum_select_fusion.refs_0_, bf16[128,4096]{1,0:T(8,128)(2,1)} %collective-permute-done.18.refs_1_, bf16[128,4096]{1,0:T(8,128)(2,1)} %collective-permute-done.19.refs_2_, bf16[128,4096]{1,0:T(8,128)(2,1)} %collective-permute-done.20.refs_3_, ...), custom_call_target="tpu_custom_call" | custom-call | tf_op jit(solution)/shard_map/project/pallas_call | solution.py:253
  247.1 8.3 %project.3 = (bf16[512,384]{1,0:T(8,128)(2,1)S(1)}, bf16[512,384]{1,0:T(8,128)(2,1)}) custom-call(bf16[128,4096]{1,0:T(8,128)(2,1)} %broadcast_select_fusion.refs_0_, bf16[128,4096]{1,0:T(8,128)(2,1)} %collective-permute-done.36.refs_1_, bf16[128,4096]{1,0:T(8,128)(2,1)} %collective-permute-done.37.refs_2_, ...), custom_call_target="tpu_custom_call" | custom-call | tf_op jit(solution)/shard_map/project/pallas_call | solution.py:253
  256.9 10.9 %collective-permute-done.39.refs_2_ = bf16[1536,384]{1,0:T(8,128)(2,1)} collective-permute-done((bf16[1536,384]{1,0:T(8,128)(2,1)}, bf16[1536,384]{1,0:T(8,128)(2,1)}, u32[]{:S(2)}, u32[]{:S(2)}) %collective-permute-start.39) | collective-permute-done | bytes 1179680 | tf_op jit(solution)/shard_map/ppermute | solution.py:125
  267.8 7.4 %collective-permute-done.40.refs_3_ = bf16[512,384]{1,0:T(8,128)(2,1)S(1)} collective-permute-done((bf16[512,384]{1,0:T(8,128)(2,1)}, bf16[512,384]{1,0:T(8,128)(2,1)S(1)}, u32[]{:S(2)}, u32[]{:S(2)}) %collective-permute-start.40) | collective-permute-done | bytes 393248 | tf_op jit(solution)/shard_map/ppermute | solution.py:125
  279.0 17.2 %flash.1 = bf16[4096,128]{1,0:T(8,128)(2,1)} custom-call(s32[33]{0:T(128)S(1)} %pad_add_fusion.1.table, bf16[1536,384]{1,0:T(8,128)(2,1)S(1)} %copy-done.9, bf16[512,384]{1,0:T(8,128)(2,1)S(1)} %copy-done.23, bf16[1536,384]{1,0:T(8,128)(2,1)} %collective-permute-done.39.refs_2_, bf16[512,384]{1,0:T(8,128)(2,1)S(1)} %collective-permute-done.40.refs_3_), custom_call_target="tpu_custom_call" | custom-call | tf_op jit(solution)/shard_map/flash/pallas_call | solution.py:206
  296.1 14.1 %all-to-all-start.3 = ((bf16[16,256,128]{2,1,0:T(8,128)(2,1)}), bf16[16,256,128]{2,1,0:T(8,128)(2,1)}, u32[]{:S(2)}, u32[]{:S(2)}) async-start(bf16[16,256,128]{2,1,0:T(8,128)(2,1)} %bitcast.20), calls=%async_computation.3 | async-start | bytes 2097152 | tf_op jit(solution)/shard_map/all_to_all | solution.py:380
  312.2 1.9 collective-permute-start.10
  319.1 28.6 %collective-permute-done.10.refs_10_ = bf16[256,2048]{1,0:T(8,128)(2,1)} collective-permute-done((bf16[256,2048]{1,0:T(8,128)(2,1)S(1)}, bf16[256,2048]{1,0:T(8,128)(2,1)}, u32[]{:S(2)}, u32[]{:S(2)}) %collective-permute-start.10) | collective-permute-done | bytes 1048608 | tf_op jit(solution)/shard_map/ppermute | solution.py:125
  347.7 21.9 %collective-permute-done.15.refs_14_ = bf16[256,2048]{1,0:T(8,128)(2,1)} collective-permute-done((bf16[256,2048]{1,0:T(8,128)(2,1)S(1)}, bf16[256,2048]{1,0:T(8,128)(2,1)}, u32[]{:S(2)}, u32[]{:S(2)}) %collective-permute-start.15) | collective-permute-done | bytes 1048608 | tf_op jit(solution)/shard_map/ppermute | solution.py:125
  373.3 23.2 %collective-permute-done.41.refs_17_ = bf16[16,256,128]{2,1,0:T(8,128)(2,1)} collective-permute-done((bf16[16,256,128]{2,1,0:T(8,128)(2,1)}, bf16[16,256,128]{2,1,0:T(8,128)(2,1)}, u32[]{:S(2)}, u32[]{:S(2)}) %collective-permute-start.41) | collective-permute-done | bytes 1048608 | tf_op jit(solution)/shard_map/ppermute | solution.py:125
  402.6 11.5 %output.1 = bf16[256,2048]{1,0:T(8,128)(2,1)} custom-call(s32[17]{0:T(128)S(1)} %concatenate.42.table, bf16[256,2048]{1,0:T(8,128)(2,1)} %refs_0_.1, bf16[256,2048]{1,0:T(8,128)(2,1)S(1)} %copy-done.11, bf16[256,2048]{1,0:T(8,128)(2,1)} %collective-permute-done.1.refs_2_, bf16[256,2048]{1,0:T(8,128)(2,1)S(1)} %copy-done.15, ...), custom_call_target="tpu_custom_call" | custom-call | tf_op jit(solution)/shard_map/output/pallas_call | solution.py:291
  (159 shorter events, 60.0 us)
Async XLA Ops:
  2.5 30.3 %all-to-all-start = ((bf16[256,16,128]{2,0,1:T(8,128)(2,1)}), bf16[256,16,128]{2,0,1:T(8,128)(2,1)S(1)}, u32[]{:S(2)}, u32[]{:S(2)}) async-start(bf16[256,16,128]{2,0,1:T(8,128)(2,1)} %copy_bitcast_fusion.2), calls=%async_computation | async-start | bytes 2097152 | tf_op jit(solution)/shard_map/all_to_all | solution.py:343
  32.8 54.1 %all-to-all-start.1 = ((bf16[256,16,128]{2,0,1:T(8,128)(2,1)}), bf16[256,16,128]{2,0,1:T(8,128)(2,1)S(1)}, u32[]{:S(2)}, u32[]{:S(2)}) async-start(bf16[256,16,128]{2,0,1:T(8,128)(2,1)} %copy_bitcast_fusion.1), calls=%async_computation.1 | async-start | bytes 2097152 | tf_op jit(solution)/shard_map/all_to_all | solution.py:343
  40.8 41.9 %collective-permute-start.21 = (bf16[128,4096]{1,0:T(8,128)(2,1)}, bf16[128,4096]{1,0:T(8,128)(2,1)}, u32[]{:S(2)}, u32[]{:S(2)}) collective-permute-start(bf16[128,4096]{1,0:T(8,128)(2,1)} %maximum_select_fusion.refs_0_), channel_id=1, source_target_pairs={{0,8},{2,10},{4,12},{6,14},{8,0},{10,2},{12,4},{14,6},{16,24},{18,... | collective-permute-start | bytes 3145736 | tf_op jit(solution)/shard_map/ppermute | solution.py:129
  42.7 41.6 %collective-permute-start.25 = (bf16[128,4096]{1,0:T(8,128)(2,1)}, bf16[128,4096]{1,0:T(8,128)(2,1)}, u32[]{:S(2)}, u32[]{:S(2)}) collective-permute-start(bf16[128,4096]{1,0:T(8,128)(2,1)} %maximum_select_fusion.refs_0_), channel_id=1, source_target_pairs={{8,16},{10,18},{12,20},{14,22},{16,8},{18,10},{20,12},{22,14},{9,1... | collective-permute-start | bytes 3145736 | tf_op jit(solution)/shard_map/ppermute | solution.py:129
  44.4 60.8 %collective-permute-start.3 = (bf16[256,2048]{1,0:T(8,128)(2,1)}, bf16[256,2048]{1,0:T(8,128)(2,1)}, u32[]{:S(2)}, u32[]{:S(2)}) collective-permute-start(bf16[256,2048]{1,0:T(8,128)(2,1)} %refs_0_.1), channel_id=1, source_target_pairs={{0,8},{2,10},{4,12},{6,14},{8,0},{10,2},{12,4},{14,6},{16,24},{18,... | collective-permute-start | bytes 3145736 | tf_op jit(solution)/shard_map/ppermute | solution.py:129
  47.6 59.0 %collective-permute-start.19 = (bf16[128,4096]{1,0:T(8,128)(2,1)}, bf16[128,4096]{1,0:T(8,128)(2,1)}, u32[]{:S(2)}, u32[]{:S(2)}) collective-permute-start(bf16[128,4096]{1,0:T(8,128)(2,1)} %maximum_select_fusion.refs_0_), channel_id=1, source_target_pairs={{0,4},{2,6},{4,0},{6,2},{8,12},{10,14},{12,8},{14,10},{16,20},{18,... | collective-permute-start | bytes 3145736 | tf_op jit(solution)/shard_map/ppermute | solution.py:125
  84.3 54.5 %collective-permute-start.26 = (bf16[128,4096]{1,0:T(8,128)(2,1)}, bf16[128,4096]{1,0:T(8,128)(2,1)}, u32[]{:S(2)}, u32[]{:S(2)}) collective-permute-start(bf16[128,4096]{1,0:T(8,128)(2,1)} %collective-permute-done.25), channel_id=1, source_target_pairs={{8,0},{10,2},{12,4},{14,6},{16,24},{18,26},{20,28},{22,30},{9,1},{... | collective-permute-start | bytes 3145736 | tf_op jit(solution)/shard_map/ppermute | solution.py:129
  86.9 59.1 %all-to-all-start.2 = ((bf16[256,16,128]{2,0,1:T(8,128)(2,1)}), bf16[256,16,128]{2,0,1:T(8,128)(2,1)S(1)}, u32[]{:S(2)}, u32[]{:S(2)}) async-start(bf16[256,16,128]{2,0,1:T(8,128)(2,1)} %copy_bitcast_fusion), calls=%async_computation.2 | async-start | bytes 2097152 | tf_op jit(solution)/shard_map/all_to_all | solution.py:343
  99.9 42.5 %collective-permute-start.18 = (bf16[128,4096]{1,0:T(8,128)(2,1)}, bf16[128,4096]{1,0:T(8,128)(2,1)}, u32[]{:S(2)}, u32[]{:S(2)}) collective-permute-start(bf16[128,4096]{1,0:T(8,128)(2,1)} %maximum_select_fusion.refs_0_), channel_id=1, source_target_pairs={{0,2},{2,0},{4,6},{6,4},{8,10},{10,8},{12,14},{14,12},{16,18},{18,... | collective-permute-start | bytes 3145736 | tf_op jit(solution)/shard_map/ppermute | solution.py:125
  105.1 38.9 %collective-permute-start.23 = (bf16[128,4096]{1,0:T(8,128)(2,1)}, bf16[128,4096]{1,0:T(8,128)(2,1)}, u32[]{:S(2)}, u32[]{:S(2)}) collective-permute-start(bf16[128,4096]{1,0:T(8,128)(2,1)} %collective-permute-done.21.refs_4_), channel_id=1, source_target_pairs={{0,4},{2,6},{4,0},{6,2},{8,12},{10,14},{12,8},{14,10},{16,20},{18,... | collective-permute-start | bytes 3145736 | tf_op jit(solution)/shard_map/ppermute | solution.py:125
  106.6 37.9 %collective-permute-start.22 = (bf16[128,4096]{1,0:T(8,128)(2,1)}, bf16[128,4096]{1,0:T(8,128)(2,1)}, u32[]{:S(2)}, u32[]{:S(2)}) collective-permute-start(bf16[128,4096]{1,0:T(8,128)(2,1)} %collective-permute-done.21.refs_4_), channel_id=1, source_target_pairs={{0,2},{2,0},{4,6},{6,4},{8,10},{10,8},{12,14},{14,12},{16,18},{18,... | collective-permute-start | bytes 3145736 | tf_op jit(solution)/shard_map/ppermute | solution.py:125
  106.7 39.3 %collective-permute-start.20 = (bf16[128,4096]{1,0:T(8,128)(2,1)}, bf16[128,4096]{1,0:T(8,128)(2,1)}, u32[]{:S(2)}, u32[]{:S(2)}) collective-permute-start(bf16[128,4096]{1,0:T(8,128)(2,1)} %collective-permute-done.19.refs_2_), channel_id=1, source_target_pairs={{0,2},{2,0},{4,6},{6,4},{8,10},{10,8},{12,14},{14,12},{16,18},{18,... | collective-permute-start | bytes 3145736 | tf_op jit(solution)/shard_map/ppermute | solution.py:125
  144.0 47.1 %collective-permute-start.31 = (bf16[4096,128]{1,0:T(8,128)(2,1)S(1)}, bf16[4096,128]{1,0:T(8,128)(2,1)}, u32[]{:S(2)}, u32[]{:S(2)}) collective-permute-start(bf16[4096,128]{1,0:T(8,128)(2,1)S(1)} %bitcast.48), channel_id=1, source_target_pairs={{0,1},{1,0},{2,3},{3,2},{4,5},{5,4},{6,7},{7,6},{8,9},{9,8},{10,11... | collective-permute-start | bytes 3145736 | tf_op jit(solution)/shard_map/ppermute | solution.py:125
  144.5 48.0 %collective-permute-start.28 = (bf16[128,4096]{1,0:T(8,128)(2,1)}, bf16[128,4096]{1,0:T(8,128)(2,1)}, u32[]{:S(2)}, u32[]{:S(2)}) collective-permute-start(bf16[128,4096]{1,0:T(8,128)(2,1)} %broadcast_select_fusion.1.refs_8_), channel_id=1, source_target_pairs={{0,4},{2,6},{4,0},{6,2},{8,12},{10,14},{12,8},{14,10},{16,20},{18,... | collective-permute-start | bytes 3145736 | tf_op jit(solution)/shard_map/ppermute | solution.py:125
  146.0 65.5 %collective-permute-start.32 = (bf16[4096,128]{1,0:T(8,128)(2,1)S(1)}, bf16[4096,128]{1,0:T(8,128)(2,1)}, u32[]{:S(2)}, u32[]{:S(2)}) collective-permute-start(bf16[4096,128]{1,0:T(8,128)(2,1)S(1)} %bitcast.51), channel_id=1, source_target_pairs={{0,1},{1,0},{2,3},{3,2},{4,5},{5,4},{6,7},{7,6},{8,9},{9,8},{10,11... | collective-permute-start | bytes 3145736 | tf_op jit(solution)/shard_map/ppermute | solution.py:125
  166.3 46.9 %collective-permute-start.27 = (bf16[128,4096]{1,0:T(8,128)(2,1)}, bf16[128,4096]{1,0:T(8,128)(2,1)}, u32[]{:S(2)}, u32[]{:S(2)}) collective-permute-start(bf16[128,4096]{1,0:T(8,128)(2,1)} %broadcast_select_fusion.1.refs_8_), channel_id=1, source_target_pairs={{0,2},{2,0},{4,6},{6,4},{8,10},{10,8},{12,14},{14,12},{16,18},{18,... | collective-permute-start | bytes 3145736 | tf_op jit(solution)/shard_map/ppermute | solution.py:125
  168.7 46.8 %collective-permute-start.24 = (bf16[128,4096]{1,0:T(8,128)(2,1)}, bf16[128,4096]{1,0:T(8,128)(2,1)S(1)}, u32[]{:S(2)}, u32[]{:S(2)}) collective-permute-start(bf16[128,4096]{1,0:T(8,128)(2,1)} %collective-permute-done.23.refs_6_), channel_id=1, source_target_pairs={{0,2},{2,0},{4,6},{6,4},{8,10},{10,8},{12,14},{14,12},{16,18},{18,... | collective-permute-start | bytes 3145736 | tf_op jit(solution)/shard_map/ppermute | solution.py:125
  211.5 28.7 %collective-permute-start.7 = (bf16[256,2048]{1,0:T(8,128)(2,1)}, bf16[256,2048]{1,0:T(8,128)(2,1)}, u32[]{:S(2)}, u32[]{:S(2)}) collective-permute-start(bf16[256,2048]{1,0:T(8,128)(2,1)} %refs_0_.1), channel_id=1, source_target_pairs={{8,16},{10,18},{12,20},{14,22},{16,8},{18,10},{20,12},{22,14},{9,1... | collective-permute-start | bytes 3145736 | tf_op jit(solution)/shard_map/ppermute | solution.py:129
  215.5 29.0 %collective-permute-start.36 = (bf16[128,4096]{1,0:T(8,128)(2,1)}, bf16[128,4096]{1,0:T(8,128)(2,1)}, u32[]{:S(2)}, u32[]{:S(2)}) collective-permute-start(bf16[128,4096]{1,0:T(8,128)(2,1)} %broadcast_select_fusion.refs_0_), channel_id=1, source_target_pairs={{0,2},{2,0},{4,6},{6,4},{8,10},{10,8},{12,14},{14,12},{16,18},{18,... | collective-permute-start | bytes 3145736 | tf_op jit(solution)/shard_map/ppermute | solution.py:125
  215.6 30.2 %collective-permute-start.38 = (bf16[128,4096]{1,0:T(8,128)(2,1)}, bf16[128,4096]{1,0:T(8,128)(2,1)}, u32[]{:S(2)}, u32[]{:S(2)}) collective-permute-start(bf16[128,4096]{1,0:T(8,128)(2,1)} %collective-permute-done.37.refs_2_), channel_id=1, source_target_pairs={{0,2},{2,0},{4,6},{6,4},{8,10},{10,8},{12,14},{14,12},{16,18},{18,... | collective-permute-start | bytes 3145736 | tf_op jit(solution)/shard_map/ppermute | solution.py:125
  238.6 29.2 %collective-permute-start.39 = (bf16[1536,384]{1,0:T(8,128)(2,1)}, bf16[1536,384]{1,0:T(8,128)(2,1)}, u32[]{:S(2)}, u32[]{:S(2)}) collective-permute-start(bf16[1536,384]{1,0:T(8,128)(2,1)} %get-tuple-element.11), channel_id=1, source_target_pairs={{0,1},{1,0},{2,3},{3,2},{4,5},{5,4},{6,7},{7,6},{8,9},{9,8},{10,11... | collective-permute-start | bytes 3538952 | tf_op jit(solution)/shard_map/ppermute | solution.py:125
  240.2 70.1 %collective-permute-start.1 = (bf16[256,2048]{1,0:T(8,128)(2,1)}, bf16[256,2048]{1,0:T(8,128)(2,1)}, u32[]{:S(2)}, u32[]{:S(2)}) collective-permute-start(bf16[256,2048]{1,0:T(8,128)(2,1)} %refs_0_.1), channel_id=1, source_target_pairs={{0,4},{2,6},{4,0},{6,2},{8,12},{10,14},{12,8},{14,10},{16,20},{18,... | collective-permute-start | bytes 3145736 | tf_op jit(solution)/shard_map/ppermute | solution.py:125
  241.7 69.0 %collective-permute-start.8 = (bf16[256,2048]{1,0:T(8,128)(2,1)}, bf16[256,2048]{1,0:T(8,128)(2,1)}, u32[]{:S(2)}, u32[]{:S(2)}) collective-permute-start(bf16[256,2048]{1,0:T(8,128)(2,1)} %collective-permute-done.7), channel_id=1, source_target_pairs={{8,0},{10,2},{12,4},{14,6},{16,24},{18,26},{20,28},{22,30},{9,1},{... | collective-permute-start | bytes 3145736 | tf_op jit(solution)/shard_map/ppermute | solution.py:129
  244.5 67.7 %collective-permute-start.13 = (bf16[256,2048]{1,0:T(8,128)(2,1)}, bf16[256,2048]{1,0:T(8,128)(2,1)}, u32[]{:S(2)}, u32[]{:S(2)}) collective-permute-start(bf16[256,2048]{1,0:T(8,128)(2,1)} %collective-permute-done.12), channel_id=1, source_target_pairs={{8,0},{10,2},{12,4},{14,6},{16,24},{18,26},{20,28},{22,30},{9,1},{... | collective-permute-start | bytes 3145736 | tf_op jit(solution)/shard_map/ppermute | solution.py:129
  267.8 47.7 %collective-permute-start = (bf16[256,2048]{1,0:T(8,128)(2,1)}, bf16[256,2048]{1,0:T(8,128)(2,1)S(1)}, u32[]{:S(2)}, u32[]{:S(2)}) collective-permute-start(bf16[256,2048]{1,0:T(8,128)(2,1)} %refs_0_.1), channel_id=1, source_target_pairs={{0,2},{2,0},{4,6},{6,4},{8,10},{10,8},{12,14},{14,12},{16,18},{18,... | collective-permute-start | bytes 3145736 | tf_op jit(solution)/shard_map/ppermute | solution.py:125
  275.2 41.4 %collective-permute-start.5 = (bf16[256,2048]{1,0:T(8,128)(2,1)}, bf16[256,2048]{1,0:T(8,128)(2,1)}, u32[]{:S(2)}, u32[]{:S(2)}) collective-permute-start(bf16[256,2048]{1,0:T(8,128)(2,1)} %collective-permute-done.3.refs_4_), channel_id=1, source_target_pairs={{0,4},{2,6},{4,0},{6,2},{8,12},{10,14},{12,8},{14,10},{16,20},{18,... | collective-permute-start | bytes 3145736 | tf_op jit(solution)/shard_map/ppermute | solution.py:125
  296.1 74.5 %all-to-all-start.3 = ((bf16[16,256,128]{2,1,0:T(8,128)(2,1)}), bf16[16,256,128]{2,1,0:T(8,128)(2,1)}, u32[]{:S(2)}, u32[]{:S(2)}) async-start(bf16[16,256,128]{2,1,0:T(8,128)(2,1)} %bitcast.20), calls=%async_computation.3 | async-start | bytes 2097152 | tf_op jit(solution)/shard_map/all_to_all | solution.py:380
  312.2 35.5 %collective-permute-start.10 = (bf16[256,2048]{1,0:T(8,128)(2,1)S(1)}, bf16[256,2048]{1,0:T(8,128)(2,1)}, u32[]{:S(2)}, u32[]{:S(2)}) collective-permute-start(bf16[256,2048]{1,0:T(8,128)(2,1)S(1)} %broadcast_select_fusion.3.refs_8_), channel_id=1, source_target_pairs={{0,4},{2,6},{4,0},{6,2},{8,12},{10,14},{12,8},{14,10},{16,20},{18,... | collective-permute-start | bytes 3145736 | tf_op jit(solution)/shard_map/ppermute | solution.py:125
  316.5 53.1 %collective-permute-start.15 = (bf16[256,2048]{1,0:T(8,128)(2,1)S(1)}, bf16[256,2048]{1,0:T(8,128)(2,1)}, u32[]{:S(2)}, u32[]{:S(2)}) collective-permute-start(bf16[256,2048]{1,0:T(8,128)(2,1)S(1)} %broadcast_select_fusion.2.refs_12_), channel_id=1, source_target_pairs={{0,4},{2,6},{4,0},{6,2},{8,12},{10,14},{12,8},{14,10},{16,20},{18,... | collective-permute-start | bytes 3145736 | tf_op jit(solution)/shard_map/ppermute | solution.py:125
  316.6 53.0 %collective-permute-start.9 = (bf16[256,2048]{1,0:T(8,128)(2,1)S(1)}, bf16[256,2048]{1,0:T(8,128)(2,1)S(1)}, u32[]{:S(2)}, u32[]{:S(2)}) collective-permute-start(bf16[256,2048]{1,0:T(8,128)(2,1)S(1)} %broadcast_select_fusion.3.refs_8_), channel_id=1, source_target_pairs={{0,2},{2,0},{4,6},{6,4},{8,10},{10,8},{12,14},{14,12},{16,18},{18,... | collective-permute-start | bytes 3145736 | tf_op jit(solution)/shard_map/ppermute | solution.py:125
  317.6 54.6 %collective-permute-start.6 = (bf16[256,2048]{1,0:T(8,128)(2,1)}, bf16[256,2048]{1,0:T(8,128)(2,1)S(1)}, u32[]{:S(2)}, u32[]{:S(2)}) collective-permute-start(bf16[256,2048]{1,0:T(8,128)(2,1)} %collective-permute-done.5.refs_6_), channel_id=1, source_target_pairs={{0,2},{2,0},{4,6},{6,4},{8,10},{10,8},{12,14},{14,12},{16,18},{18,... | collective-permute-start | bytes 3145736 | tf_op jit(solution)/shard_map/ppermute | solution.py:125
  319.1 54.1 %collective-permute-start.14 = (bf16[256,2048]{1,0:T(8,128)(2,1)S(1)}, bf16[256,2048]{1,0:T(8,128)(2,1)}, u32[]{:S(2)}, u32[]{:S(2)}) collective-permute-start(bf16[256,2048]{1,0:T(8,128)(2,1)S(1)} %broadcast_select_fusion.2.refs_12_), channel_id=1, source_target_pairs={{0,2},{2,0},{4,6},{6,4},{8,10},{10,8},{12,14},{14,12},{16,18},{18,... | collective-permute-start | bytes 3145736 | tf_op jit(solution)/shard_map/ppermute | solution.py:125
  (44 other events, 658.9 us)
where the time goes:
time: 416 us; the launch traced here: 414 us
  waiting for transfers between devices  234 us (56%)
  starting transfers between devices  78.1 us (19%)
  Pallas kernels  57.1 us (14%)
  local copies, waits for them, and re-layouts  29.5 us (7%)
  other arithmetic  15.4 us (4%)
    ppermute x32, waiting for transfers between devices, exchanged(): return lax.ppermute(x, axis, [(i, i ^ bit) for i in range(peers)])  127 us
    ppermute x10, waiting for transfers between devices, sent(): return lax.ppermute(x, 'ctx', pairs)  89.2 us
    pallas_call x2, Pallas kernels, project(): pl.pallas_call(functools.partial(project_kernel, head_dim=head_dim), grid...  28.5 us
    ppermute x32, starting transfers between devices, exchanged(): return lax.ppermute(x, axis, [(i, i ^ bit) for i in range(peers)])  23.9 us
    all_to_all x3, starting transfers between devices, swap(): lax.all_to_all(weight, 'ctx', split_axis=1, concat_axis=0, tiled=True)  22.9 us
    unnamed x60, local copies, waits for them, and re-layouts  18.8 us
    all_to_all x3, waiting for transfers between devices, swap(): lax.all_to_all(weight, 'ctx', split_axis=1, concat_axis=0, tiled=True)  17.9 us
    ppermute x10, starting transfers between devices, sent(): return lax.ppermute(x, 'ctx', pairs)  17.2 us
  transfers between devices with their start and end apart: 46, of which 13 were waited for; matrix products, arithmetic and copies ran while one was open for 6% of the time, Pallas kernels for 11%

commit v1 on v0

--- a/solution.py
+++ b/solution.py
@@ -151,21 +151,20 @@
     return [z_index, z_index ^ 1, jnp.where(low, 2, 1), jnp.where(low, 3, 0)]
 
 
-def flash_kernel(table, *refs, head_dim, block, piece):
+def flash_kernel(table, *refs, plan, head_dim, block, piece):
     *parts, out, query, key, value = refs
-    own, peer = parts[: len(parts) // 2], parts[len(parts) // 2 :]
+    targets = (query, key, value)
     slab_len = query.shape[0]
-    entry = 0
-    for pair in zip(own, peer):
-        for part in range(pair[0].shape[0] // piece):
+    for at, (first, kinds) in enumerate(plan):
+        for part in range(parts[2 * at].shape[0] // piece):
             rows = slice(part * piece, (part + 1) * piece)
-            for source in pair:
-                place = pl.ds(pl.multiple_of(table[entry] * piece, piece), piece)
-                query[place, :] = source[rows, :head_dim]
-                key[place, :] = source[rows, head_dim : 2 * head_dim]
-                value[place, :] = source[rows, 2 * head_dim :]
-                entry += 1
-    offset = table[entry]
+            for side in range(2):
+                number = table[(first * 4 + part) * 2 + side]
+                place = pl.ds(pl.multiple_of(number * piece, piece), piece)
+                for inner, kind in enumerate(kinds):
+                    columns = slice(inner * head_dim, (inner + 1) * head_dim)
+                    targets[kind][place, :] = parts[2 * at + side][rows, columns]
+    offset = table[2 * (slab_len // (2 * piece))]
     scale = head_dim ** (-0.5) * 1.4426950408889634
     diagonal = lax.broadcasted_iota(jnp.int32, (block, block), 1) <= lax.broadcasted_iota(
         jnp.int32, (block, block), 0
@@ -199,24 +198,25 @@
         out[pl.ds(pl.multiple_of(start, block), block), :] = (mixed / total).astype(jnp.bfloat16)
 
 
-def flash(table, own, peer, slab_len, head_dim, piece, block=256):
-    body = functools.partial(flash_kernel, head_dim=head_dim, block=block, piece=piece)
+def flash(table, parts, plan, slab_len, head_dim, piece, block=256):
+    body = functools.partial(flash_kernel, plan=plan, head_dim=head_dim, block=block, piece=piece)
     vmem = pl.BlockSpec(memory_space=pltpu.VMEM)
     scratch = [pltpu.VMEM((slab_len, head_dim), jnp.bfloat16)] * 3
     return pl.pallas_call(
         body,
         out_shape=jax.ShapeDtypeStruct((slab_len, head_dim), jnp.bfloat16),
-        in_specs=[pl.BlockSpec(memory_space=pltpu.SMEM)] + [vmem] * (2 * len(own)),
+        in_specs=[pl.BlockSpec(memory_space=pltpu.SMEM)] + [vmem] * len(parts),
         out_specs=vmem,
         scratch_shapes=scratch,
         compiler_params=pltpu.CompilerParams(vmem_limit_bytes=48 * 2**20),
         name="flash",
-    )(table, *own, *peer)
-
-
-def project_kernel(*refs, head_dim):
+    )(table, *parts)
+
+
+def project_kernel(*refs, kinds, head_dim):
     *inputs, down, up, cosine, sine, mine, other, total = refs
-    pieces, weights = inputs[:-6], inputs[-6:]
+    count = len(kinds)
+    pieces, weights = inputs[: -2 * count], inputs[-2 * count :]
     step = pl.program_id(0)
     rows = jnp.concatenate([piece[...] for piece in pieces], 0)
 
@@ -225,41 +225,41 @@
         total[...] = jnp.zeros_like(total)
 
     wide = 2 * head_dim
-    for which in range(3):
-        pair = jnp.concatenate([weights[which][...], weights[which + 3][...]], 1)
+    for which in range(count):
+        pair = jnp.concatenate([weights[which][...], weights[which + count][...]], 1)
         total[:, which * wide : (which + 1) * wide] += fold_rows(rows, pair)
-    total[:, 3 * wide :] += fold_rows(rows, down[...])
+    total[:, count * wide :] += fold_rows(rows, down[...])
 
     @pl.when(step == pl.num_programs(0) - 1)
     def _():
-        low = total[:, 3 * wide :].astype(jnp.bfloat16)
-        for which in range(3):
+        low = total[:, count * wide :].astype(jnp.bfloat16)
+        for which, kind in enumerate(kinds):
             for side, out in enumerate((mine, other)):
                 start = which * wide + side * head_dim
                 proj = total[:, start : start + head_dim] + 2.0 * fold_rows(
-                    low, up[:, start : start + head_dim]
+                    low, up[:, kind * wide + side * head_dim : kind * wide + (side + 1) * head_dim]
                 )
-                if which < 2:
+                if kind < 2:
                     turned = pltpu.roll(proj, head_dim // 2, 1)
                     proj = proj * cosine[...] + turned * sine[...]
                 out[:, which * head_dim : (which + 1) * head_dim] = proj.astype(jnp.bfloat16)
 
 
-def project(pieces, weights, down, up, cosine, sine, head_dim, depth=1024):
+def project(pieces, weights, kinds, down, up, cosine, sine, head_dim, depth=512):
     rows = sum(piece.shape[0] for piece in pieces)
     width = weights[0].shape[0]
     whole = lambda shape: pl.BlockSpec(shape, lambda k: (0, 0))
-    out = jax.ShapeDtypeStruct((rows, 3 * head_dim), jnp.bfloat16)
+    out = jax.ShapeDtypeStruct((rows, len(kinds) * head_dim), jnp.bfloat16)
     return pl.pallas_call(
-        functools.partial(project_kernel, head_dim=head_dim),
+        functools.partial(project_kernel, kinds=kinds, head_dim=head_dim),
         grid=(width // depth,),
         out_shape=(out, out),
         in_specs=[pl.BlockSpec((piece.shape[0], depth), lambda k: (0, k)) for piece in pieces]
-        + [pl.BlockSpec((depth, head_dim), lambda k: (k, 0))] * 6
+        + [pl.BlockSpec((depth, head_dim), lambda k: (k, 0))] * len(weights)
         + [pl.BlockSpec((depth, down.shape[1]), lambda k: (k, 0))]
         + [whole(up.shape), whole(cosine.shape), whole(sine.shape)],
         out_specs=[whole(out.shape)] * 2,
-        scratch_shapes=[pltpu.VMEM((rows, 6 * head_dim + down.shape[1]), jnp.float32)],
+        scratch_shapes=[pltpu.VMEM((rows, 2 * len(kinds) * head_dim + down.shape[1]), jnp.float32)],
         compiler_params=pltpu.CompilerParams(vmem_limit_bytes=40 * 2**20),
         name="project",
     )(*pieces, *weights, down, up, cosine, sine)
@@ -343,7 +343,7 @@
         return lax.all_to_all(weight, "ctx", split_axis=1, concat_axis=0, tiled=True)
 
     mine = [swap(weight) for weight in (query_weight, key_weight, value_weight)]
-    pair_weights = mine + [exchanged(weight, "head", 1) for weight in mine]
+    others = [exchanged(weight, "head", 1) for weight in mine]
 
     down = jnp.pad(adapter_down.reshape(3 * rank, D).T, ((0, 0), (0, head_dim - 3 * rank)))
     up_mine = lax.dynamic_slice_in_dim(adapter_up, ctx_index * head_dim, head_dim, 2)
@@ -356,8 +356,8 @@
     local = jnp.arange(half, dtype=jnp.int32)
     inverse_freq = 10000.0 ** (-(jnp.arange(head_dim // 2, dtype=jnp.float32) * 2.0) / head_dim)
     places = [z * plane + (in_plane ^ variant) for z in line_sources(z_index)]
-    own_parts, peer_parts = [], []
-    for first, last in GROUPS:
+    parts, plan = [], []
+    for first, last, split in GROUPS:
         rows_from = jnp.concatenate(places[first:last])[:, None] * tok_rows
         positions = (rows_from + y_index * half + local[None, :]).reshape(-1)
         angles = positions.astype(jnp.float32)[:, None] * inverse_freq[None, :]
@@ -365,9 +365,13 @@
         cosine = jnp.concatenate([cosine, cosine], 1)
         sine = jnp.concatenate([-sine, sine], 1)
         pieces = [piece for slot in slots[first:last] for piece in slot]
-        own_part, peer_part = project(pieces, pair_weights, down, up, cosine, sine, head_dim)
-        own_parts.append(own_part)
-        peer_parts.append(exchanged(peer_part, "head", 1))
+        for kinds in split:
+            weights = [mine[kind] for kind in kinds] + [others[kind] for kind in kinds]
+            own_part, peer_part = project(
+                pieces, weights, kinds, down, up, cosine, sine, head_dim
+            )
+            parts += [own_part, exchanged(peer_part, "head", 1)]
+            plan.append((first, kinds))
 
     sources = jnp.concatenate(places)
     shift = jnp.where(y_index * ctx_count + ctx_index >= HEADS // 2, slab_len // 2, 0)
@@ -375,7 +379,7 @@
     table = (sources[:, None] * 2 + sides[None, :]).reshape(-1)
     table = (table - shift // half) % (slab_len // half)
     table = jnp.concatenate([table, shift[None]]).astype(jnp.int32)
-    result = flash(table, own_parts, peer_parts, slab_len, head_dim, half)
+    result = flash(table, parts, plan, slab_len, head_dim, half)
     blocks = result.reshape(ctx_count, tok_rows, head_dim)
     mixed = lax.all_to_all(blocks, "ctx", split_axis=0, concat_axis=0, tiled=True)
     mixed_other = exchanged(mixed, "head", 1)
@@ -386,7 +390,7 @@
     return output_project(out_table, pieces, mixed, mixed_other)
 
 
-GROUPS = ((0, 3), (3, 4))
+GROUPS = ((0, 3, ((0, 1), (2,))), (3, 4, ((0, 1, 2),)))
 
 
 def one_head_fits(mesh):

time: 416 us -> 409 us (0.983)
  waiting for transfers between devices: 234 us -> 187 us
  starting transfers between devices: 78.1 us -> 95.3 us
  Pallas kernels: 57.1 us -> 67.6 us
  local copies, waits for them, and re-layouts: 29.5 us -> 39.7 us
    all_to_all x3, starting transfers between devices: 22.9 us -> 47.9 us  [swap(): lax.all_to_all(weight, 'ctx', split_axis=1, concat_axis=0, tiled=True)]
    ppermute x10, waiting for transfers between devices: 89.2 us -> 68.1 us  [sent(): return lax.ppermute(x, 'ctx', pairs)]
    all_to_all x3, waiting for transfers between devices: 17.9 us -> 3.18 us  [swap(): lax.all_to_all(weight, 'ctx', split_axis=1, concat_axis=0, tiled=True)]
    pallas_call x2 -> x3, Pallas kernels: 28.5 us -> 39.3 us  [project(): pl.pallas_call(functools.partial(project_kernel, kinds=kinds, head_dim=he...]
    ppermute x32 -> x33, waiting for transfers between devices: 127 us -> 116 us  [exchanged(): return lax.ppermute(x, axis, [(i, i ^ bit) for i in range(peers)])]
    unnamed x60 -> x90, local copies, waits for them, and re-layouts: 18.8 us -> 29.1 us
    all_to_all x1, starting transfers between devices: 14.1 us -> 6.12 us  [attention_layer(): lax.all_to_all(blocks, 'ctx', split_axis=0, concat_axis=0, tiled=True)]
    ppermute x32 -> x33, starting transfers between devices: 23.9 us -> 25.6 us  [exchanged(): return lax.ppermute(x, axis, [(i, i ^ bit) for i in range(peers)])]
  transfers between devices with their start and end apart: 46 -> 47, of which waited for: 13 -> 13; matrix products, arithmetic and copies ran while one was open for 6% -> 6% of each run, Pallas kernels for 11% -> 14%
where the time goes in v1:
time: 409 us; the launch traced here: 407 us
  waiting for transfers between devices  187 us (46%)
  starting transfers between devices  95.3 us (23%)
  Pallas kernels  67.6 us (17%)
  local copies, waits for them, and re-layouts  39.7 us (10%)
  other arithmetic  16.6 us (4%)
    ppermute x33, waiting for transfers between devices, exchanged(): return lax.ppermute(x, axis, [(i, i ^ bit) for i in range(peers)])  116 us
    ppermute x10, waiting for transfers between devices, sent(): return lax.ppermute(x, 'ctx', pairs)  68.1 us
    all_to_all x3, starting transfers between devices, swap(): lax.all_to_all(weight, 'ctx', split_axis=1, concat_axis=0, tiled=True)  47.9 us
    pallas_call x3, Pallas kernels, project(): pl.pallas_call(functools.partial(project_kernel, kinds=kinds, head_dim=he...  39.3 us
    unnamed x90, local copies, waits for them, and re-layouts  29.1 us
    ppermute x33, starting transfers between devices, exchanged(): return lax.ppermute(x, axis, [(i, i ^ bit) for i in range(peers)])  25.6 us
    pallas_call x1, Pallas kernels, flash(): pl.pallas_call(body, out_shape=jax.ShapeDtypeStruct((slab_len, head_dim),...  16.8 us
    ppermute x10, starting transfers between devices, sent(): return lax.ppermute(x, 'ctx', pairs)  15.7 us
  transfers between devices with their start and end apart: 47, of which 13 were waited for; matrix products, arithmetic and copies ran while one was open for 6% of the time, Pallas kernels for 14%

profile of v1, /device:TPU:0, one launch (start us, length us, event | category | flops | bytes accessed | tf_op | source)
XLA Modules:
  0.0 407.2 jit_solution(12802568165206347354)
XLA Ops:
  2.5 7.5 %all-to-all-start = ((bf16[256,16,128]{2,0,1:T(8,128)(2,1)}), bf16[256,16,128]{2,0,1:T(8,128)(2,1)S(1)}, u32[]{:S(2)}, u32[]{:S(2)}) async-start(bf16[256,16,128]{2,0,1:T(8,128)(2,1)} %copy_bitcast_fusion.2), calls=%async_computation | async-start | bytes 2097152 | tf_op jit(solution)/shard_map/all_to_all | solution.py:343
  12.4 12.9 %collective-permute-done.17 = bf16[128,2048]{1,0:T(8,128)(2,1)S(1)} collective-permute-done((bf16[128,2048]{1,0:T(8,128)(2,1)}, bf16[128,2048]{1,0:T(8,128)(2,1)S(1)}, u32[]{:S(2)}, u32[]{:S(2)}) %collective-permute-start.17) | collective-permute-done | bytes 524320 | tf_op jit(solution)/shard_map/ppermute | solution.py:125
  25.6 1.7 collective-permute-start.21
  30.2 3.2 all-to-all-done
  33.4 6.9 %all-to-all-start.2 = ((bf16[256,16,128]{2,0,1:T(8,128)(2,1)}), bf16[256,16,128]{2,0,1:T(8,128)(2,1)S(1)}, u32[]{:S(2)}, u32[]{:S(2)}) async-start(bf16[256,16,128]{2,0,1:T(8,128)(2,1)} %copy_bitcast_fusion), calls=%async_computation.2 | async-start | bytes 2097152 | tf_op jit(solution)/shard_map/all_to_all | solution.py:343
  42.5 1.9 collective-permute-start.3
  47.5 9.4 %collective-permute-done.21.refs_4_ = bf16[128,4096]{1,0:T(8,128)(2,1)} collective-permute-done((bf16[128,4096]{1,0:T(8,128)(2,1)S(1)}, bf16[128,4096]{1,0:T(8,128)(2,1)}, u32[]{:S(2)}, u32[]{:S(2)}) %collective-permute-start.21) | collective-permute-done | bytes 1048608 | tf_op jit(solution)/shard_map/ppermute | solution.py:129
  56.9 1.7 collective-permute-start.36
  59.9 2.5 copy_bitcast_fusion.1
  62.4 31.6 %collective-permute-done.3.refs_4_ = bf16[256,2048]{1,0:T(8,128)(2,1)} collective-permute-done((bf16[256,2048]{1,0:T(8,128)(2,1)}, bf16[256,2048]{1,0:T(8,128)(2,1)}, u32[]{:S(2)}, u32[]{:S(2)}) %collective-permute-start.3) | collective-permute-done | bytes 1048608 | tf_op jit(solution)/shard_map/ppermute | solution.py:129
  94.0 2.8 collective-permute-start.23
  98.3 33.5 %all-to-all-start.1 = ((bf16[256,16,128]{2,0,1:T(8,128)(2,1)}), bf16[256,16,128]{2,0,1:T(8,128)(2,1)}, u32[]{:S(2)}, u32[]{:S(2)}) async-start(bf16[256,16,128]{2,0,1:T(8,128)(2,1)} %copy_bitcast_fusion.1), calls=%async_computation.1 | async-start | bytes 2097152 | tf_op jit(solution)/shard_map/all_to_all | solution.py:343
  136.9 27.1 %collective-permute-done.37 = bf16[128,4096]{1,0:T(8,128)(2,1)} collective-permute-done((bf16[128,4096]{1,0:T(8,128)(2,1)}, bf16[128,4096]{1,0:T(8,128)(2,1)}, u32[]{:S(2)}, u32[]{:S(2)}) %collective-permute-start.37) | collective-permute-done | bytes 1048608 | tf_op jit(solution)/shard_map/ppermute | solution.py:129
  164.0 2.3 broadcast_select_fusion.refs_0_
  168.3 4.5 %fusion = (f32[1536,64]{1,0:T(8,128)}, f32[1536,64]{1,0:T(8,128)}, f32[1536,64]{1,0:T(8,128)}) fusion(f32[64]{0:T(128)S(1)} %multiply_power_fusion, f32[1536]{0:T(1024)S(1)} %convert_bitcast_fusion), kind=kLoop, calls=%fused_computation.16 | loop fusion | flops 196608 | bytes 1186048 | tf_op jit(solution)/shard_map/neg | solution.py:366
  172.8 1.8 collective-permute-start.12
  177.7 2.5 pad_maximum_fusion.refs_18_.refs_16_
  180.2 12.1 %collective-permute-done.39.refs_2_ = bf16[128,4096]{1,0:T(8,128)(2,1)} collective-permute-done((bf16[128,4096]{1,0:T(8,128)(2,1)}, bf16[128,4096]{1,0:T(8,128)(2,1)}, u32[]{:S(2)}, u32[]{:S(2)}) %collective-permute-start.39) | collective-permute-done | bytes 1048608 | tf_op jit(solution)/shard_map/ppermute | solution.py:125
  194.8 2.6 pad.5.refs_16_.refs_14_.refs_10_
  201.7 12.5 %project.4 = (bf16[1536,128]{1,0:T(8,128)(2,1)S(1)}, bf16[1536,128]{1,0:T(8,128)(2,1)}) custom-call(bf16[128,4096]{1,0:T(8,128)(2,1)S(1)} %maximum_select_fusion.refs_0_, bf16[128,4096]{1,0:T(8,128)(2,1)} %collective-permute-done.18.refs_1_, bf16[128,4096]{1,0:T(8,128)(2,1)} %collective-permute-done.19.refs_2_, bf16[128,4096]{1,0:T(8,128)(2,1)S(1)} %copy-done.16, ...), custom_call_target="tpu_custom_call" | custom-call | tf_op jit(solution)/shard_map/project/pallas_call | solution.py:253
  217.8 5.9 %collective-permute-done.31.refs_15_.refs_8_ = bf16[4096,128]{1,0:T(8,128)(2,1)} collective-permute-done((bf16[4096,128]{1,0:T(8,128)(2,1)}, bf16[4096,128]{1,0:T(8,128)(2,1)}, u32[]{:S(2)}, u32[]{:S(2)}) %collective-permute-start.31) | collective-permute-done | bytes 1048608 | tf_op jit(solution)/shard_map/ppermute | solution.py:125
  231.1 16.5 %project.3 = (bf16[1536,256]{1,0:T(8,128)(2,1)S(1)}, bf16[1536,256]{1,0:T(8,128)(2,1)}) custom-call(bf16[128,4096]{1,0:T(8,128)(2,1)S(1)} %maximum_select_fusion.refs_0_, bf16[128,4096]{1,0:T(8,128)(2,1)} %collective-permute-done.18.refs_1_, bf16[128,4096]{1,0:T(8,128)(2,1)} %collective-permute-done.19.refs_2_, bf16[128,4096]{1,0:T(8,128)(2,1)S(1)} %copy-done.17, ...), custom_call_target="tpu_custom_call" | custom-call | tf_op jit(solution)/shard_map/project/pallas_call | solution.py:253
  250.8 10.3 %project.5 = (bf16[512,384]{1,0:T(8,128)(2,1)S(1)}, bf16[512,384]{1,0:T(8,128)(2,1)}) custom-call(bf16[128,4096]{1,0:T(8,128)(2,1)} %broadcast_select_fusion.refs_0_, bf16[128,4096]{1,0:T(8,128)(2,1)} %collective-permute-done.38.refs_1_, bf16[128,4096]{1,0:T(8,128)(2,1)} %collective-permute-done.39.refs_2_, ...), custom_call_target="tpu_custom_call" | custom-call | tf_op jit(solution)/shard_map/project/pallas_call | solution.py:253
  263.6 5.7 %collective-permute-done.33.refs_1_ = bf16[1536,256]{1,0:T(8,128)(2,1)S(1)} collective-permute-done((bf16[1536,256]{1,0:T(8,128)(2,1)}, bf16[1536,256]{1,0:T(8,128)(2,1)S(1)}, u32[]{:S(2)}, u32[]{:S(2)}) %collective-permute-start.33) | collective-permute-done | bytes 786464 | tf_op jit(solution)/shard_map/ppermute | solution.py:125
  270.1 5.9 %collective-permute-done.41.refs_5_ = bf16[512,384]{1,0:T(8,128)(2,1)S(1)} collective-permute-done((bf16[512,384]{1,0:T(8,128)(2,1)}, bf16[512,384]{1,0:T(8,128)(2,1)S(1)}, u32[]{:S(2)}, u32[]{:S(2)}) %collective-permute-start.41) | collective-permute-done | bytes 393248 | tf_op jit(solution)/shard_map/ppermute | solution.py:125
  280.2 16.8 %flash.1 = bf16[4096,128]{1,0:T(8,128)(2,1)} custom-call(s32[33]{0:T(128)S(1)} %pad_add_fusion.1.table, bf16[1536,256]{1,0:T(8,128)(2,1)S(1)} %copy-done.32, bf16[1536,256]{1,0:T(8,128)(2,1)S(1)} %copy-done.34, bf16[1536,128]{1,0:T(8,128)(2,1)S(1)} %copy-done.36, bf16[1536,128]{1,0:T(8,128)(2,1)} %collective-permute-done.35.refs_3_, ...), custom_call_target="tpu_custom_call" | custom-call | tf_op jit(solution)/shard_map/flash/pallas_call | solution.py:205
  297.1 6.1 %all-to-all-start.3 = ((bf16[16,256,128]{2,1,0:T(8,128)(2,1)}), bf16[16,256,128]{2,1,0:T(8,128)(2,1)}, u32[]{:S(2)}, u32[]{:S(2)}) async-start(bf16[16,256,128]{2,1,0:T(8,128)(2,1)} %bitcast.20), calls=%async_computation.3 | async-start | bytes 2097152 | tf_op jit(solution)/shard_map/all_to_all | solution.py:384
  306.1 1.9 collective-permute-start.10
  313.0 27.6 %collective-permute-done.10.refs_10_ = bf16[256,2048]{1,0:T(8,128)(2,1)} collective-permute-done((bf16[256,2048]{1,0:T(8,128)(2,1)S(1)}, bf16[256,2048]{1,0:T(8,128)(2,1)}, u32[]{:S(2)}, u32[]{:S(2)}) %collective-permute-start.10) | collective-permute-done | bytes 1048608 | tf_op jit(solution)/shard_map/ppermute | solution.py:125
  340.6 21.9 %collective-permute-done.15.refs_14_ = bf16[256,2048]{1,0:T(8,128)(2,1)} collective-permute-done((bf16[256,2048]{1,0:T(8,128)(2,1)S(1)}, bf16[256,2048]{1,0:T(8,128)(2,1)}, u32[]{:S(2)}, u32[]{:S(2)}) %collective-permute-start.15) | collective-permute-done | bytes 1048608 | tf_op jit(solution)/shard_map/ppermute | solution.py:125
  365.8 23.6 %collective-permute-done.42.refs_17_ = bf16[16,256,128]{2,1,0:T(8,128)(2,1)} collective-permute-done((bf16[16,256,128]{2,1,0:T(8,128)(2,1)}, bf16[16,256,128]{2,1,0:T(8,128)(2,1)}, u32[]{:S(2)}, u32[]{:S(2)}) %collective-permute-start.42) | collective-permute-done | bytes 1048608 | tf_op jit(solution)/shard_map/ppermute | solution.py:125
  395.6 11.5 %output.1 = bf16[256,2048]{1,0:T(8,128)(2,1)} custom-call(s32[17]{0:T(128)S(1)} %concatenate.42.table, bf16[256,2048]{1,0:T(8,128)(2,1)} %refs_0_.1, bf16[256,2048]{1,0:T(8,128)(2,1)S(1)} %copy-done.22, bf16[256,2048]{1,0:T(8,128)(2,1)} %collective-permute-done.1.refs_2_, bf16[256,2048]{1,0:T(8,128)(2,1)S(1)} %copy-done.26, ...), custom_call_target="tpu_custom_call" | custom-call | tf_op jit(solution)/shard_map/output/pallas_call | solution.py:291
  (192 shorter events, 71.8 us)
Async XLA Ops:
  33.4 64.9 %all-to-all-start.2 = ((bf16[256,16,128]{2,0,1:T(8,128)(2,1)}), bf16[256,16,128]{2,0,1:T(8,128)(2,1)S(1)}, u32[]{:S(2)}, u32[]{:S(2)}) async-start(bf16[256,16,128]{2,0,1:T(8,128)(2,1)} %copy_bitcast_fusion), calls=%async_computation.2 | async-start | bytes 2097152 | tf_op jit(solution)/shard_map/all_to_all | solution.py:343
  42.5 51.5 %collective-permute-start.3 = (bf16[256,2048]{1,0:T(8,128)(2,1)}, bf16[256,2048]{1,0:T(8,128)(2,1)}, u32[]{:S(2)}, u32[]{:S(2)}) collective-permute-start(bf16[256,2048]{1,0:T(8,128)(2,1)} %refs_0_.1), channel_id=1, source_target_pairs={{0,8},{2,10},{4,12},{6,14},{8,0},{10,2},{12,4},{14,6},{16,24},{18,... | collective-permute-start | bytes 3145736 | tf_op jit(solution)/shard_map/ppermute | solution.py:129
  44.4 49.6 %collective-permute-start.7 = (bf16[256,2048]{1,0:T(8,128)(2,1)}, bf16[256,2048]{1,0:T(8,128)(2,1)}, u32[]{:S(2)}, u32[]{:S(2)}) collective-permute-start(bf16[256,2048]{1,0:T(8,128)(2,1)} %refs_0_.1), channel_id=1, source_target_pairs={{8,16},{10,18},{12,20},{14,22},{16,8},{18,10},{20,12},{22,14},{9,1... | collective-permute-start | bytes 3145736 | tf_op jit(solution)/shard_map/ppermute | solution.py:129
  46.1 50.7 %collective-permute-start.19 = (bf16[128,4096]{1,0:T(8,128)(2,1)S(1)}, bf16[128,4096]{1,0:T(8,128)(2,1)}, u32[]{:S(2)}, u32[]{:S(2)}) collective-permute-start(bf16[128,4096]{1,0:T(8,128)(2,1)S(1)} %maximum_select_fusion.refs_0_), channel_id=1, source_target_pairs={{0,4},{2,6},{4,0},{6,2},{8,12},{10,14},{12,8},{14,10},{16,20},{18,... | collective-permute-start | bytes 3145736 | tf_op jit(solution)/shard_map/ppermute | solution.py:125
  56.9 40.1 %collective-permute-start.36 = (bf16[128,4096]{1,0:T(8,128)(2,1)}, bf16[128,4096]{1,0:T(8,128)(2,1)}, u32[]{:S(2)}, u32[]{:S(2)}) collective-permute-start(bf16[128,4096]{1,0:T(8,128)(2,1)} %collective-permute-done.21.refs_4_), channel_id=1, source_target_pairs={{8,16},{10,18},{12,20},{14,22},{16,8},{18,10},{20,12},{22,14},{9,1... | collective-permute-start | bytes 3145736 | tf_op jit(solution)/shard_map/ppermute | solution.py:129
  58.6 73.3 %collective-permute-start.26 = (bf16[128,4096]{1,0:T(8,128)(2,1)}, bf16[128,4096]{1,0:T(8,128)(2,1)}, u32[]{:S(2)}, u32[]{:S(2)}) collective-permute-start(bf16[128,4096]{1,0:T(8,128)(2,1)} %collective-permute-done.25), channel_id=1, source_target_pairs={{8,0},{10,2},{12,4},{14,6},{16,24},{18,26},{20,28},{22,30},{9,1},{... | collective-permute-start | bytes 3145736 | tf_op jit(solution)/shard_map/ppermute | solution.py:129
  94.0 39.7 %collective-permute-start.18 = (bf16[128,4096]{1,0:T(8,128)(2,1)S(1)}, bf16[128,4096]{1,0:T(8,128)(2,1)}, u32[]{:S(2)}, u32[]{:S(2)}) collective-permute-start(bf16[128,4096]{1,0:T(8,128)(2,1)S(1)} %maximum_select_fusion.refs_0_), channel_id=1, source_target_pairs={{0,2},{2,0},{4,6},{6,4},{8,10},{10,8},{12,14},{14,12},{16,18},{18,... | collective-permute-start | bytes 3145736 | tf_op jit(solution)/shard_map/ppermute | solution.py:125
  94.0 41.3 %collective-permute-start.23 = (bf16[128,4096]{1,0:T(8,128)(2,1)}, bf16[128,4096]{1,0:T(8,128)(2,1)}, u32[]{:S(2)}, u32[]{:S(2)}) collective-permute-start(bf16[128,4096]{1,0:T(8,128)(2,1)} %collective-permute-done.21.refs_4_), channel_id=1, source_target_pairs={{0,4},{2,6},{4,0},{6,2},{8,12},{10,14},{12,8},{14,10},{16,20},{18,... | collective-permute-start | bytes 3145736 | tf_op jit(solution)/shard_map/ppermute | solution.py:125
  96.8 40.1 %collective-permute-start.22 = (bf16[128,4096]{1,0:T(8,128)(2,1)}, bf16[128,4096]{1,0:T(8,128)(2,1)}, u32[]{:S(2)}, u32[]{:S(2)}) collective-permute-start(bf16[128,4096]{1,0:T(8,128)(2,1)} %collective-permute-done.21.refs_4_), channel_id=1, source_target_pairs={{0,2},{2,0},{4,6},{6,4},{8,10},{10,8},{12,14},{14,12},{16,18},{18,... | collective-permute-start | bytes 3145736 | tf_op jit(solution)/shard_map/ppermute | solution.py:125
  97.0 67.0 %collective-permute-start.37 = (bf16[128,4096]{1,0:T(8,128)(2,1)}, bf16[128,4096]{1,0:T(8,128)(2,1)}, u32[]{:S(2)}, u32[]{:S(2)}) collective-permute-start(bf16[128,4096]{1,0:T(8,128)(2,1)} %collective-permute-done.36), channel_id=1, source_target_pairs={{8,0},{10,2},{12,4},{14,6},{16,24},{18,26},{20,28},{22,30},{9,1},{... | collective-permute-start | bytes 3145736 | tf_op jit(solution)/shard_map/ppermute | solution.py:129
  98.3 78.8 %all-to-all-start.1 = ((bf16[256,16,128]{2,0,1:T(8,128)(2,1)}), bf16[256,16,128]{2,0,1:T(8,128)(2,1)}, u32[]{:S(2)}, u32[]{:S(2)}) async-start(bf16[256,16,128]{2,0,1:T(8,128)(2,1)} %copy_bitcast_fusion.1), calls=%async_computation.1 | async-start | bytes 2097152 | tf_op jit(solution)/shard_map/all_to_all | solution.py:343
  131.9 34.5 %collective-permute-start.20 = (bf16[128,4096]{1,0:T(8,128)(2,1)}, bf16[128,4096]{1,0:T(8,128)(2,1)S(1)}, u32[]{:S(2)}, u32[]{:S(2)}) collective-permute-start(bf16[128,4096]{1,0:T(8,128)(2,1)} %collective-permute-done.19.refs_2_), channel_id=1, source_target_pairs={{0,2},{2,0},{4,6},{6,4},{8,10},{10,8},{12,14},{14,12},{16,18},{18,... | collective-permute-start | bytes 3145736 | tf_op jit(solution)/shard_map/ppermute | solution.py:125
  133.7 39.1 %collective-permute-start.34 = (bf16[4096,128]{1,0:T(8,128)(2,1)S(1)}, bf16[4096,128]{1,0:T(8,128)(2,1)S(1)}, u32[]{:S(2)}, u32[]{:S(2)}) collective-permute-start(bf16[4096,128]{1,0:T(8,128)(2,1)S(1)} %bitcast.48), channel_id=1, source_target_pairs={{0,1},{1,0},{2,3},{3,2},{4,5},{5,4},{6,7},{7,6},{8,9},{9,8},{10,11... | collective-permute-start | bytes 3145736 | tf_op jit(solution)/shard_map/ppermute | solution.py:125
  135.2 33.0 %collective-permute-start.28 = (bf16[128,4096]{1,0:T(8,128)(2,1)S(1)}, bf16[128,4096]{1,0:T(8,128)(2,1)}, u32[]{:S(2)}, u32[]{:S(2)}) collective-permute-start(bf16[128,4096]{1,0:T(8,128)(2,1)S(1)} %broadcast_select_fusion.1.refs_8_), channel_id=1, source_target_pairs={{0,4},{2,6},{4,0},{6,2},{8,12},{10,14},{12,8},{14,10},{16,20},{18,... | collective-permute-start | bytes 3145736 | tf_op jit(solution)/shard_map/ppermute | solution.py:125
  136.9 37.7 %collective-permute-start.27 = (bf16[128,4096]{1,0:T(8,128)(2,1)S(1)}, bf16[128,4096]{1,0:T(8,128)(2,1)S(1)}, u32[]{:S(2)}, u32[]{:S(2)}) collective-permute-start(bf16[128,4096]{1,0:T(8,128)(2,1)S(1)} %broadcast_select_fusion.1.refs_8_), channel_id=1, source_target_pairs={{0,2},{2,0},{4,6},{6,4},{8,10},{10,8},{12,14},{14,12},{16,18},{18,... | collective-permute-start | bytes 3145736 | tf_op jit(solution)/shard_map/ppermute | solution.py:125
  172.8 42.2 %collective-permute-start.12 = (bf16[256,2048]{1,0:T(8,128)(2,1)}, bf16[256,2048]{1,0:T(8,128)(2,1)}, u32[]{:S(2)}, u32[]{:S(2)}) collective-permute-start(bf16[256,2048]{1,0:T(8,128)(2,1)} %collective-permute-done.3.refs_4_), channel_id=1, source_target_pairs={{8,16},{10,18},{12,20},{14,22},{16,8},{18,10},{20,12},{22,14},{9,1... | collective-permute-start | bytes 3145736 | tf_op jit(solution)/shard_map/ppermute | solution.py:129
  175.6 40.7 %collective-permute-start.30 = (bf16[4096,128]{1,0:T(8,128)(2,1)S(1)}, bf16[4096,128]{1,0:T(8,128)(2,1)}, u32[]{:S(2)}, u32[]{:S(2)}) collective-permute-start(bf16[4096,128]{1,0:T(8,128)(2,1)S(1)} %bitcast.45), channel_id=1, source_target_pairs={{0,1},{1,0},{2,3},{3,2},{4,5},{5,4},{6,7},{7,6},{8,9},{9,8},{10,11... | collective-permute-start | bytes 3145736 | tf_op jit(solution)/shard_map/ppermute | solution.py:125
  177.1 46.6 %collective-permute-start.31 = (bf16[4096,128]{1,0:T(8,128)(2,1)}, bf16[4096,128]{1,0:T(8,128)(2,1)}, u32[]{:S(2)}, u32[]{:S(2)}) collective-permute-start(bf16[4096,128]{1,0:T(8,128)(2,1)} %bitcast.7.refs_13_.refs_5_), channel_id=1, source_target_pairs={{0,1},{1,0},{2,3},{3,2},{4,5},{5,4},{6,7},{7,6},{8,9},{9,8},{10,11... | collective-permute-start | bytes 3145736 | tf_op jit(solution)/shard_map/ppermute | solution.py:125
  192.3 56.3 %collective-permute-start.38 = (bf16[128,4096]{1,0:T(8,128)(2,1)}, bf16[128,4096]{1,0:T(8,128)(2,1)}, u32[]{:S(2)}, u32[]{:S(2)}) collective-permute-start(bf16[128,4096]{1,0:T(8,128)(2,1)} %broadcast_select_fusion.refs_0_), channel_id=1, source_target_pairs={{0,2},{2,0},{4,6},{6,4},{8,10},{10,8},{12,14},{14,12},{16,18},{18,... | collective-permute-start | bytes 3145736 | tf_op jit(solution)/shard_map/ppermute | solution.py:125
  197.4 52.0 %collective-permute-start.40 = (bf16[128,4096]{1,0:T(8,128)(2,1)}, bf16[128,4096]{1,0:T(8,128)(2,1)}, u32[]{:S(2)}, u32[]{:S(2)}) collective-permute-start(bf16[128,4096]{1,0:T(8,128)(2,1)} %collective-permute-done.39.refs_2_), channel_id=1, source_target_pairs={{0,2},{2,0},{4,6},{6,4},{8,10},{10,8},{12,14},{14,12},{16,18},{18,... | collective-permute-start | bytes 3145736 | tf_op jit(solution)/shard_map/ppermute | solution.py:125
  215.0 88.2 %collective-permute-start.1 = (bf16[256,2048]{1,0:T(8,128)(2,1)}, bf16[256,2048]{1,0:T(8,128)(2,1)}, u32[]{:S(2)}, u32[]{:S(2)}) collective-permute-start(bf16[256,2048]{1,0:T(8,128)(2,1)} %refs_0_.1), channel_id=1, source_target_pairs={{0,4},{2,6},{4,0},{6,2},{8,12},{10,14},{12,8},{14,10},{16,20},{18,... | collective-permute-start | bytes 3145736 | tf_op jit(solution)/shard_map/ppermute | solution.py:125
  216.3 87.3 %collective-permute-start.8 = (bf16[256,2048]{1,0:T(8,128)(2,1)}, bf16[256,2048]{1,0:T(8,128)(2,1)}, u32[]{:S(2)}, u32[]{:S(2)}) collective-permute-start(bf16[256,2048]{1,0:T(8,128)(2,1)} %collective-permute-done.7), channel_id=1, source_target_pairs={{8,0},{10,2},{12,4},{14,6},{16,24},{18,26},{20,28},{22,30},{9,1},{... | collective-permute-start | bytes 3145736 | tf_op jit(solution)/shard_map/ppermute | solution.py:129
  223.8 38.0 %collective-permute-start.35 = (bf16[1536,128]{1,0:T(8,128)(2,1)}, bf16[1536,128]{1,0:T(8,128)(2,1)}, u32[]{:S(2)}, u32[]{:S(2)}) collective-permute-start(bf16[1536,128]{1,0:T(8,128)(2,1)} %get-tuple-element.14), channel_id=1, source_target_pairs={{0,1},{1,0},{2,3},{3,2},{4,5},{5,4},{6,7},{7,6},{8,9},{9,8},{10,11... | collective-permute-start | bytes 1179656 | tf_op jit(solution)/shard_map/ppermute | solution.py:125
  249.4 55.7 %collective-permute-start.13 = (bf16[256,2048]{1,0:T(8,128)(2,1)}, bf16[256,2048]{1,0:T(8,128)(2,1)S(1)}, u32[]{:S(2)}, u32[]{:S(2)}) collective-permute-start(bf16[256,2048]{1,0:T(8,128)(2,1)} %collective-permute-done.12), channel_id=1, source_target_pairs={{8,0},{10,2},{12,4},{14,6},{16,24},{18,26},{20,28},{22,30},{9,1},{... | collective-permute-start | bytes 3145736 | tf_op jit(solution)/shard_map/ppermute | solution.py:129
  270.1 39.2 %collective-permute-start = (bf16[256,2048]{1,0:T(8,128)(2,1)}, bf16[256,2048]{1,0:T(8,128)(2,1)S(1)}, u32[]{:S(2)}, u32[]{:S(2)}) collective-permute-start(bf16[256,2048]{1,0:T(8,128)(2,1)} %refs_0_.1), channel_id=1, source_target_pairs={{0,2},{2,0},{4,6},{6,4},{8,10},{10,8},{12,14},{14,12},{16,18},{18,... | collective-permute-start | bytes 3145736 | tf_op jit(solution)/shard_map/ppermute | solution.py:125
  276.1 34.4 %collective-permute-start.5 = (bf16[256,2048]{1,0:T(8,128)(2,1)}, bf16[256,2048]{1,0:T(8,128)(2,1)}, u32[]{:S(2)}, u32[]{:S(2)}) collective-permute-start(bf16[256,2048]{1,0:T(8,128)(2,1)} %collective-permute-done.3.refs_4_), channel_id=1, source_target_pairs={{0,4},{2,6},{4,0},{6,2},{8,12},{10,14},{12,8},{14,10},{16,20},{18,... | collective-permute-start | bytes 3145736 | tf_op jit(solution)/shard_map/ppermute | solution.py:125
  297.1 66.5 %all-to-all-start.3 = ((bf16[16,256,128]{2,1,0:T(8,128)(2,1)}), bf16[16,256,128]{2,1,0:T(8,128)(2,1)}, u32[]{:S(2)}, u32[]{:S(2)}) async-start(bf16[16,256,128]{2,1,0:T(8,128)(2,1)} %bitcast.20), calls=%async_computation.3 | async-start | bytes 2097152 | tf_op jit(solution)/shard_map/all_to_all | solution.py:384
  306.1 34.5 %collective-permute-start.10 = (bf16[256,2048]{1,0:T(8,128)(2,1)S(1)}, bf16[256,2048]{1,0:T(8,128)(2,1)}, u32[]{:S(2)}, u32[]{:S(2)}) collective-permute-start(bf16[256,2048]{1,0:T(8,128)(2,1)S(1)} %broadcast_select_fusion.3.refs_8_), channel_id=1, source_target_pairs={{0,4},{2,6},{4,0},{6,2},{8,12},{10,14},{12,8},{14,10},{16,20},{18,... | collective-permute-start | bytes 3145736 | tf_op jit(solution)/shard_map/ppermute | solution.py:125
  310.3 52.2 %collective-permute-start.15 = (bf16[256,2048]{1,0:T(8,128)(2,1)S(1)}, bf16[256,2048]{1,0:T(8,128)(2,1)}, u32[]{:S(2)}, u32[]{:S(2)}) collective-permute-start(bf16[256,2048]{1,0:T(8,128)(2,1)S(1)} %broadcast_select_fusion.2.refs_12_), channel_id=1, source_target_pairs={{0,4},{2,6},{4,0},{6,2},{8,12},{10,14},{12,8},{14,10},{16,20},{18,... | collective-permute-start | bytes 3145736 | tf_op jit(solution)/shard_map/ppermute | solution.py:125
  310.5 52.1 %collective-permute-start.9 = (bf16[256,2048]{1,0:T(8,128)(2,1)S(1)}, bf16[256,2048]{1,0:T(8,128)(2,1)S(1)}, u32[]{:S(2)}, u32[]{:S(2)}) collective-permute-start(bf16[256,2048]{1,0:T(8,128)(2,1)S(1)} %broadcast_select_fusion.3.refs_8_), channel_id=1, source_target_pairs={{0,2},{2,0},{4,6},{6,4},{8,10},{10,8},{12,14},{14,12},{16,18},{18,... | collective-permute-start | bytes 3145736 | tf_op jit(solution)/shard_map/ppermute | solution.py:125
  311.4 53.4 %collective-permute-start.6 = (bf16[256,2048]{1,0:T(8,128)(2,1)}, bf16[256,2048]{1,0:T(8,128)(2,1)S(1)}, u32[]{:S(2)}, u32[]{:S(2)}) collective-permute-start(bf16[256,2048]{1,0:T(8,128)(2,1)} %collective-permute-done.5.refs_6_), channel_id=1, source_target_pairs={{0,2},{2,0},{4,6},{6,4},{8,10},{10,8},{12,14},{14,12},{16,18},{18,... | collective-permute-start | bytes 3145736 | tf_op jit(solution)/shard_map/ppermute | solution.py:125
  313.0 52.8 %collective-permute-start.14 = (bf16[256,2048]{1,0:T(8,128)(2,1)S(1)}, bf16[256,2048]{1,0:T(8,128)(2,1)}, u32[]{:S(2)}, u32[]{:S(2)}) collective-permute-start(bf16[256,2048]{1,0:T(8,128)(2,1)S(1)} %broadcast_select_fusion.2.refs_12_), channel_id=1, source_target_pairs={{0,2},{2,0},{4,6},{6,4},{8,10},{10,8},{12,14},{14,12},{16,18},{18,... | collective-permute-start | bytes 3145736 | tf_op jit(solution)/shard_map/ppermute | solution.py:125
  (60 other events, 686.0 us)

commit v2 on v1

--- a/solution.py
+++ b/solution.py
@@ -213,39 +213,69 @@
     )(table, *parts)
 
 
+def lower_kernel(*refs):
+    *pieces, down, out, total = refs
+    step = pl.program_id(0)
+
+    @pl.when(step == 0)
+    def _():
+        total[...] = jnp.zeros_like(total)
+
+    rows = jnp.concatenate([piece[...] for piece in pieces], 0)
+    total[...] += fold_rows(rows, down[...])
+
+    @pl.when(step == pl.num_programs(0) - 1)
+    def _():
+        out[...] = total[...].astype(jnp.bfloat16)
+
+
+def lower(pieces, down, depth=512):
+    rows = sum(piece.shape[0] for piece in pieces)
+    width, rank = down.shape
+    return pl.pallas_call(
+        lower_kernel,
+        grid=(width // depth,),
+        out_shape=jax.ShapeDtypeStruct((rows, rank), jnp.bfloat16),
+        in_specs=[pl.BlockSpec((piece.shape[0], depth), lambda k: (0, k)) for piece in pieces]
+        + [pl.BlockSpec((depth, rank), lambda k: (k, 0))],
+        out_specs=pl.BlockSpec((rows, rank), lambda k: (0, 0)),
+        scratch_shapes=[pltpu.VMEM((rows, rank), jnp.float32)],
+        compiler_params=pltpu.CompilerParams(vmem_limit_bytes=40 * 2**20),
+        name="lower",
+    )(*pieces, down)
+
+
 def project_kernel(*refs, kinds, head_dim):
-    *inputs, down, up, cosine, sine, mine, other, total = refs
+    *inputs, low, up, cosine, sine, mine, other, total = refs
     count = len(kinds)
     pieces, weights = inputs[: -2 * count], inputs[-2 * count :]
     step = pl.program_id(0)
-    rows = jnp.concatenate([piece[...] for piece in pieces], 0)
+    wide = 2 * head_dim
 
     @pl.when(step == 0)
     def _():
         total[...] = jnp.zeros_like(total)
 
-    wide = 2 * head_dim
+    rows = jnp.concatenate([piece[...] for piece in pieces], 0)
     for which in range(count):
         pair = jnp.concatenate([weights[which][...], weights[which + count][...]], 1)
         total[:, which * wide : (which + 1) * wide] += fold_rows(rows, pair)
-    total[:, count * wide :] += fold_rows(rows, down[...])
 
     @pl.when(step == pl.num_programs(0) - 1)
     def _():
-        low = total[:, count * wide :].astype(jnp.bfloat16)
         for which, kind in enumerate(kinds):
+            added = fold_rows(low[...], up[:, kind * wide : (kind + 1) * wide])
             for side, out in enumerate((mine, other)):
                 start = which * wide + side * head_dim
-                proj = total[:, start : start + head_dim] + 2.0 * fold_rows(
-                    low, up[:, kind * wide + side * head_dim : kind * wide + (side + 1) * head_dim]
-                )
+                proj = total[:, start : start + head_dim]
+                proj = proj + 2.0 * added[:, side * head_dim : (side + 1) * head_dim]
                 if kind < 2:
                     turned = pltpu.roll(proj, head_dim // 2, 1)
                     proj = proj * cosine[...] + turned * sine[...]
                 out[:, which * head_dim : (which + 1) * head_dim] = proj.astype(jnp.bfloat16)
 
 
-def project(pieces, weights, kinds, down, up, cosine, sine, head_dim, depth=512):
+def project(pieces, weights, kinds, low, up, cosine, sine, head_dim, depth):
     rows = sum(piece.shape[0] for piece in pieces)
     width = weights[0].shape[0]
     whole = lambda shape: pl.BlockSpec(shape, lambda k: (0, 0))
@@ -256,13 +286,12 @@
         out_shape=(out, out),
         in_specs=[pl.BlockSpec((piece.shape[0], depth), lambda k: (0, k)) for piece in pieces]
         + [pl.BlockSpec((depth, head_dim), lambda k: (k, 0))] * len(weights)
-        + [pl.BlockSpec((depth, down.shape[1]), lambda k: (k, 0))]
-        + [whole(up.shape), whole(cosine.shape), whole(sine.shape)],
+        + [whole(low.shape), whole(up.shape), whole(cosine.shape), whole(sine.shape)],
         out_specs=[whole(out.shape)] * 2,
-        scratch_shapes=[pltpu.VMEM((rows, 2 * len(kinds) * head_dim + down.shape[1]), jnp.float32)],
+        scratch_shapes=[pltpu.VMEM((rows, 2 * len(kinds) * head_dim), jnp.float32)],
         compiler_params=pltpu.CompilerParams(vmem_limit_bytes=40 * 2**20),
         name="project",
-    )(*pieces, *weights, down, up, cosine, sine)
+    )(*pieces, *weights, low, up, cosine, sine)
 
 
 def output_kernel(table, *refs):
@@ -365,10 +394,13 @@
         cosine = jnp.concatenate([cosine, cosine], 1)
         sine = jnp.concatenate([-sine, sine], 1)
         pieces = [piece for slot in slots[first:last] for piece in slot]
+        ready, cosine, sine, full_up = lax.optimization_barrier((down, cosine, sine, up))
+        low = lower(pieces, ready)
         for kinds in split:
             weights = [mine[kind] for kind in kinds] + [others[kind] for kind in kinds]
+            depth = 512 if len(kinds) == 2 else 1024
             own_part, peer_part = project(
-                pieces, weights, kinds, down, up, cosine, sine, head_dim
+                pieces, weights, kinds, low, full_up, cosine, sine, head_dim, depth
             )
             parts += [own_part, exchanged(peer_part, "head", 1)]
             plan.append((first, kinds))

time: 409 us -> 406 us (level)
  local copies, waits for them, and re-layouts: 39.7 us -> 29.7 us
    pallas_call x0 -> x2, Pallas kernels: none -> 14.2 us  [lower(): pl.pallas_call(lower_kernel, grid=(width // depth,), out_shape=jax.ShapeD...]
    pallas_call x3, Pallas kernels: 39.3 us -> 28.2 us  [project(): pl.pallas_call(functools.partial(project_kernel, kinds=kinds, head_dim=he...]
    unnamed x90 -> x92, local copies, waits for them, and re-layouts: 29.1 us -> 20.8 us
  transfers between devices with their start and end apart: 47 -> 47, of which waited for: 13 -> 14; matrix products, arithmetic and copies ran while one was open for 6% -> 6% of each run, Pallas kernels for 14% -> 15%
where the time goes in v2:
time: 406 us; the launch traced here: 404 us
  waiting for transfers between devices  188 us (46%)
  starting transfers between devices  97.3 us (24%)
  Pallas kernels  70.8 us (17%)
  local copies, waits for them, and re-layouts  29.7 us (7%)
  other arithmetic  17.4 us (4%)
    ppermute x33, waiting for transfers between devices, exchanged(): return lax.ppermute(x, axis, [(i, i ^ bit) for i in range(peers)])  118 us
    ppermute x10, waiting for transfers between devices, sent(): return lax.ppermute(x, 'ctx', pairs)  65.8 us
    all_to_all x3, starting transfers between devices, swap(): lax.all_to_all(weight, 'ctx', split_axis=1, concat_axis=0, tiled=True)  48.6 us
    pallas_call x3, Pallas kernels, project(): pl.pallas_call(functools.partial(project_kernel, kinds=kinds, head_dim=he...  28.2 us
    ppermute x33, starting transfers between devices, exchanged(): return lax.ppermute(x, axis, [(i, i ^ bit) for i in range(peers)])  25.7 us
    unnamed x92, local copies, waits for them, and re-layouts  20.8 us
    pallas_call x1, Pallas kernels, flash(): pl.pallas_call(body, out_shape=jax.ShapeDtypeStruct((slab_len, head_dim),...  16.9 us
    ppermute x10, starting transfers between devices, sent(): return lax.ppermute(x, 'ctx', pairs)  15.5 us
  transfers between devices with their start and end apart: 47, of which 14 were waited for; matrix products, arithmetic and copies ran while one was open for 6% of the time, Pallas kernels for 15%

profile of v2, /device:TPU:0, one launch (start us, length us, event | category | flops | bytes accessed | tf_op | source)
XLA Modules:
  0.0 404.0 jit_solution(17578918937613004560)
XLA Ops:
  2.5 7.6 %all-to-all-start = ((bf16[256,16,128]{2,0,1:T(8,128)(2,1)}), bf16[256,16,128]{2,0,1:T(8,128)(2,1)}, u32[]{:S(2)}, u32[]{:S(2)}) async-start(bf16[256,16,128]{2,0,1:T(8,128)(2,1)} %copy_bitcast_fusion.2), calls=%async_computation | async-start | bytes 2097152 | tf_op jit(solution)/shard_map/all_to_all | solution.py:372
  11.8 12.7 %collective-permute-done.17 = bf16[128,2048]{1,0:T(8,128)(2,1)S(1)} collective-permute-done((bf16[128,2048]{1,0:T(8,128)(2,1)S(1)}, bf16[128,2048]{1,0:T(8,128)(2,1)S(1)}, u32[]{:S(2)}, u32[]{:S(2)}) %collective-permute-start.17) | collective-permute-done | bytes 524320 | tf_op jit(solution)/shard_map/ppermute | solution.py:125
  29.3 4.2 %all-to-all-done = bf16[256,16,128]{2,0,1:T(8,128)(2,1)} async-done(((bf16[256,16,128]{2,0,1:T(8,128)(2,1)}), bf16[256,16,128]{2,0,1:T(8,128)(2,1)}, u32[]{:S(2)}, u32[]{:S(2)}) %all-to-all-start) | async-done | bytes 1048608 | tf_op jit(solution)/shard_map/all_to_all | solution.py:372
  33.5 6.9 %all-to-all-start.2 = ((bf16[256,16,128]{2,0,1:T(8,128)(2,1)}), bf16[256,16,128]{2,0,1:T(8,128)(2,1)S(1)}, u32[]{:S(2)}, u32[]{:S(2)}) async-start(bf16[256,16,128]{2,0,1:T(8,128)(2,1)} %copy_bitcast_fusion), calls=%async_computation.2 | async-start | bytes 2097152 | tf_op jit(solution)/shard_map/all_to_all | solution.py:372
  42.7 1.9 collective-permute-start.3
  47.7 5.9 %collective-permute-done.21.refs_4_ = bf16[128,4096]{1,0:T(8,128)(2,1)S(1)} collective-permute-done((bf16[128,4096]{1,0:T(8,128)(2,1)S(1)}, bf16[128,4096]{1,0:T(8,128)(2,1)S(1)}, u32[]{:S(2)}, u32[]{:S(2)}) %collective-permute-start.21) | collective-permute-done | bytes 1048608 | tf_op jit(solution)/shard_map/ppermute | solution.py:129
  56.6 2.5 copy_bitcast_fusion.1
  59.1 33.9 %collective-permute-done.3.refs_4_ = bf16[256,2048]{1,0:T(8,128)(2,1)} collective-permute-done((bf16[256,2048]{1,0:T(8,128)(2,1)}, bf16[256,2048]{1,0:T(8,128)(2,1)}, u32[]{:S(2)}, u32[]{:S(2)}) %collective-permute-start.3) | collective-permute-done | bytes 1048608 | tf_op jit(solution)/shard_map/ppermute | solution.py:129
  93.0 3.1 collective-permute-start.23
  98.7 34.1 %all-to-all-start.1 = ((bf16[256,16,128]{2,0,1:T(8,128)(2,1)}), bf16[256,16,128]{2,0,1:T(8,128)(2,1)}, u32[]{:S(2)}, u32[]{:S(2)}) async-start(bf16[256,16,128]{2,0,1:T(8,128)(2,1)} %copy_bitcast_fusion.1), calls=%async_computation.1 | async-start | bytes 2097152 | tf_op jit(solution)/shard_map/all_to_all | solution.py:372
  138.0 26.0 %collective-permute-done.37 = bf16[128,4096]{1,0:T(8,128)(2,1)} collective-permute-done((bf16[128,4096]{1,0:T(8,128)(2,1)}, bf16[128,4096]{1,0:T(8,128)(2,1)}, u32[]{:S(2)}, u32[]{:S(2)}) %collective-permute-start.37) | collective-permute-done | bytes 1048608 | tf_op jit(solution)/shard_map/ppermute | solution.py:129
  164.0 2.3 broadcast_select_fusion.refs_0_
  167.9 1.9 collective-permute-done.28.refs_10_
  169.8 4.5 %fusion = (f32[1536,64]{1,0:T(8,128)}, f32[1536,64]{1,0:T(8,128)}, f32[1536,64]{1,0:T(8,128)}) fusion(f32[64]{0:T(128)S(1)} %multiply_power_fusion, f32[1536]{0:T(1024)S(1)} %convert_bitcast_fusion), kind=kLoop, calls=%fused_computation.16 | loop fusion | flops 196608 | bytes 1186048 | tf_op jit(solution)/shard_map/neg | solution.py:395
  179.0 2.5 pad_maximum_fusion.refs_18_.refs_16_
  181.5 10.7 %collective-permute-done.39.refs_2_ = bf16[128,4096]{1,0:T(8,128)(2,1)} collective-permute-done((bf16[128,4096]{1,0:T(8,128)(2,1)}, bf16[128,4096]{1,0:T(8,128)(2,1)}, u32[]{:S(2)}, u32[]{:S(2)}) %collective-permute-start.39) | collective-permute-done | bytes 1048608 | tf_op jit(solution)/shard_map/ppermute | solution.py:125
  197.1 8.2 %lower.2.refs_16_.refs_14_ = bf16[1536,128]{1,0:T(8,128)(2,1)S(1)} custom-call(bf16[128,4096]{1,0:T(8,128)(2,1)S(1)} %maximum_select_fusion.refs_0_, bf16[128,4096]{1,0:T(8,128)(2,1)} %collective-permute-done.18.refs_1_, bf16[128,4096]{1,0:T(8,128)(2,1)} %collective-permute-done.19.refs_2_, bf16[128,4096]{1,0:T(8,128)(2,1)S(1)} %copy-done.3, ...), custom_call_target="tpu_custom_call" | custom-call | tf_op jit(solution)/shard_map/lower/pallas_call | solution.py:235
  205.4 7.7 %project.4 = (bf16[1536,128]{1,0:T(8,128)(2,1)S(1)}, bf16[1536,128]{1,0:T(8,128)(2,1)}) custom-call(bf16[128,4096]{1,0:T(8,128)(2,1)S(1)} %maximum_select_fusion.refs_0_, bf16[128,4096]{1,0:T(8,128)(2,1)} %collective-permute-done.18.refs_1_, bf16[128,4096]{1,0:T(8,128)(2,1)} %collective-permute-done.19.refs_2_, bf16[128,4096]{1,0:T(8,128)(2,1)S(1)} %copy-done.3, ...), custom_call_target="tpu_custom_call" | custom-call | tf_op jit(solution)/shard_map/project/pallas_call | solution.py:283
  216.7 8.5 %collective-permute-done.31.refs_15_.refs_8_ = bf16[4096,128]{1,0:T(8,128)(2,1)} collective-permute-done((bf16[4096,128]{1,0:T(8,128)(2,1)}, bf16[4096,128]{1,0:T(8,128)(2,1)}, u32[]{:S(2)}, u32[]{:S(2)}) %collective-permute-start.31) | collective-permute-done | bytes 1048608 | tf_op jit(solution)/shard_map/ppermute | solution.py:125
  226.8 1.9 fusion.1
  234.4 13.0 %project.3 = (bf16[1536,256]{1,0:T(8,128)(2,1)S(1)}, bf16[1536,256]{1,0:T(8,128)(2,1)}) custom-call(bf16[128,4096]{1,0:T(8,128)(2,1)S(1)} %maximum_select_fusion.refs_0_, bf16[128,4096]{1,0:T(8,128)(2,1)} %collective-permute-done.18.refs_1_, bf16[128,4096]{1,0:T(8,128)(2,1)} %collective-permute-done.19.refs_2_, bf16[128,4096]{1,0:T(8,128)(2,1)S(1)} %copy-done.4, ...), custom_call_target="tpu_custom_call" | custom-call | tf_op jit(solution)/shard_map/project/pallas_call | solution.py:283
  249.7 6.0 %lower.3.refs_10_ = bf16[512,128]{1,0:T(8,128)(2,1)S(1)} custom-call(bf16[128,4096]{1,0:T(8,128)(2,1)} %broadcast_select_fusion.refs_0_, bf16[128,4096]{1,0:T(8,128)(2,1)} %collective-permute-done.38.refs_1_, bf16[128,4096]{1,0:T(8,128)(2,1)} %collective-permute-done.39.refs_2_, bf16[128,4096]{1,0:T(8,128)(2,1)} %collective-permute-done.40.refs_3_, ...), custom_call_target="tpu_custom_call" | custom-call | tf_op jit(solution)/shard_map/lower/pallas_call | solution.py:235
  255.7 7.6 %project.5 = (bf16[512,384]{1,0:T(8,128)(2,1)S(1)}, bf16[512,384]{1,0:T(8,128)(2,1)}) custom-call(bf16[128,4096]{1,0:T(8,128)(2,1)} %broadcast_select_fusion.refs_0_, bf16[128,4096]{1,0:T(8,128)(2,1)} %collective-permute-done.38.refs_1_, bf16[128,4096]{1,0:T(8,128)(2,1)} %collective-permute-done.39.refs_2_, ...), custom_call_target="tpu_custom_call" | custom-call | tf_op jit(solution)/shard_map/project/pallas_call | solution.py:283
  265.2 2.1 collective-permute-done.33.refs_1_
  267.3 7.6 %collective-permute-done.41.refs_5_ = bf16[512,384]{1,0:T(8,128)(2,1)} collective-permute-done((bf16[512,384]{1,0:T(8,128)(2,1)}, bf16[512,384]{1,0:T(8,128)(2,1)}, u32[]{:S(2)}, u32[]{:S(2)}) %collective-permute-start.41) | collective-permute-done | bytes 393248 | tf_op jit(solution)/shard_map/ppermute | solution.py:125
  275.7 16.9 %flash.1 = bf16[4096,128]{1,0:T(8,128)(2,1)} custom-call(s32[33]{0:T(128)S(1)} %pad_add_fusion.1.table, bf16[1536,256]{1,0:T(8,128)(2,1)S(1)} %copy-done.33, bf16[1536,256]{1,0:T(8,128)(2,1)S(1)} %collective-permute-done.33.refs_1_, bf16[1536,128]{1,0:T(8,128)(2,1)S(1)} %copy-done.35, bf16[1536,128]{1,0:T(8,128)(2,1)} %collective-permute-done.35.refs_3_, ...), custom_call_target="tpu_custom_call" | custom-call | tf_op jit(solution)/shard_map/flash/pallas_call | solution.py:205
  292.6 7.5 %all-to-all-start.3 = ((bf16[16,256,128]{2,1,0:T(8,128)(2,1)}), bf16[16,256,128]{2,1,0:T(8,128)(2,1)}, u32[]{:S(2)}, u32[]{:S(2)}) async-start(bf16[16,256,128]{2,1,0:T(8,128)(2,1)} %bitcast.20), calls=%async_computation.3 | async-start | bytes 2097152 | tf_op jit(solution)/shard_map/all_to_all | solution.py:416
  302.0 1.9 collective-permute-start.10
  308.9 28.6 %collective-permute-done.10.refs_10_ = bf16[256,2048]{1,0:T(8,128)(2,1)} collective-permute-done((bf16[256,2048]{1,0:T(8,128)(2,1)S(1)}, bf16[256,2048]{1,0:T(8,128)(2,1)}, u32[]{:S(2)}, u32[]{:S(2)}) %collective-permute-start.10) | collective-permute-done | bytes 1048608 | tf_op jit(solution)/shard_map/ppermute | solution.py:125
  337.5 21.9 %collective-permute-done.15.refs_14_ = bf16[256,2048]{1,0:T(8,128)(2,1)} collective-permute-done((bf16[256,2048]{1,0:T(8,128)(2,1)S(1)}, bf16[256,2048]{1,0:T(8,128)(2,1)}, u32[]{:S(2)}, u32[]{:S(2)}) %collective-permute-start.15) | collective-permute-done | bytes 1048608 | tf_op jit(solution)/shard_map/ppermute | solution.py:125
  362.4 23.9 %collective-permute-done.42.refs_17_ = bf16[16,256,128]{2,1,0:T(8,128)(2,1)} collective-permute-done((bf16[16,256,128]{2,1,0:T(8,128)(2,1)}, bf16[16,256,128]{2,1,0:T(8,128)(2,1)}, u32[]{:S(2)}, u32[]{:S(2)}) %collective-permute-start.42) | collective-permute-done | bytes 1048608 | tf_op jit(solution)/shard_map/ppermute | solution.py:125
  392.4 11.5 %output.1 = bf16[256,2048]{1,0:T(8,128)(2,1)} custom-call(s32[17]{0:T(128)S(1)} %concatenate.42.table, bf16[256,2048]{1,0:T(8,128)(2,1)} %refs_0_.1, bf16[256,2048]{1,0:T(8,128)(2,1)S(1)} %copy-done.23, bf16[256,2048]{1,0:T(8,128)(2,1)} %collective-permute-done.1.refs_2_, bf16[256,2048]{1,0:T(8,128)(2,1)S(1)} %copy-done.27, ...), custom_call_target="tpu_custom_call" | custom-call | tf_op jit(solution)/shard_map/output/pallas_call | solution.py:320
  (196 shorter events, 68.0 us)
Async XLA Ops:
  33.5 64.2 %all-to-all-start.2 = ((bf16[256,16,128]{2,0,1:T(8,128)(2,1)}), bf16[256,16,128]{2,0,1:T(8,128)(2,1)S(1)}, u32[]{:S(2)}, u32[]{:S(2)}) async-start(bf16[256,16,128]{2,0,1:T(8,128)(2,1)} %copy_bitcast_fusion), calls=%async_computation.2 | async-start | bytes 2097152 | tf_op jit(solution)/shard_map/all_to_all | solution.py:372
  42.7 50.4 %collective-permute-start.3 = (bf16[256,2048]{1,0:T(8,128)(2,1)}, bf16[256,2048]{1,0:T(8,128)(2,1)}, u32[]{:S(2)}, u32[]{:S(2)}) collective-permute-start(bf16[256,2048]{1,0:T(8,128)(2,1)} %refs_0_.1), channel_id=1, source_target_pairs={{0,8},{2,10},{4,12},{6,14},{8,0},{10,2},{12,4},{14,6},{16,24},{18,... | collective-permute-start | bytes 3145736 | tf_op jit(solution)/shard_map/ppermute | solution.py:129
  44.6 48.4 %collective-permute-start.7 = (bf16[256,2048]{1,0:T(8,128)(2,1)}, bf16[256,2048]{1,0:T(8,128)(2,1)}, u32[]{:S(2)}, u32[]{:S(2)}) collective-permute-start(bf16[256,2048]{1,0:T(8,128)(2,1)} %refs_0_.1), channel_id=1, source_target_pairs={{8,16},{10,18},{12,20},{14,22},{16,8},{18,10},{20,12},{22,14},{9,1... | collective-permute-start | bytes 3145736 | tf_op jit(solution)/shard_map/ppermute | solution.py:129
  46.2 49.9 %collective-permute-start.19 = (bf16[128,4096]{1,0:T(8,128)(2,1)S(1)}, bf16[128,4096]{1,0:T(8,128)(2,1)}, u32[]{:S(2)}, u32[]{:S(2)}) collective-permute-start(bf16[128,4096]{1,0:T(8,128)(2,1)S(1)} %maximum_select_fusion.refs_0_), channel_id=1, source_target_pairs={{0,4},{2,6},{4,0},{6,2},{8,12},{10,14},{12,8},{14,10},{16,20},{18,... | collective-permute-start | bytes 3145736 | tf_op jit(solution)/shard_map/ppermute | solution.py:125
  53.6 42.8 %collective-permute-start.36 = (bf16[128,4096]{1,0:T(8,128)(2,1)S(1)}, bf16[128,4096]{1,0:T(8,128)(2,1)}, u32[]{:S(2)}, u32[]{:S(2)}) collective-permute-start(bf16[128,4096]{1,0:T(8,128)(2,1)S(1)} %collective-permute-done.21.refs_4_), channel_id=1, source_target_pairs={{8,16},{10,18},{12,20},{14,22},{16,8},{18,10},{20,12},{22,14},{9,1... | collective-permute-start | bytes 3145736 | tf_op jit(solution)/shard_map/ppermute | solution.py:129
  55.2 77.7 %collective-permute-start.26 = (bf16[128,4096]{1,0:T(8,128)(2,1)}, bf16[128,4096]{1,0:T(8,128)(2,1)}, u32[]{:S(2)}, u32[]{:S(2)}) collective-permute-start(bf16[128,4096]{1,0:T(8,128)(2,1)} %collective-permute-done.25), channel_id=1, source_target_pairs={{8,0},{10,2},{12,4},{14,6},{16,24},{18,26},{20,28},{22,30},{9,1},{... | collective-permute-start | bytes 3145736 | tf_op jit(solution)/shard_map/ppermute | solution.py:129
  93.0 41.7 %collective-permute-start.18 = (bf16[128,4096]{1,0:T(8,128)(2,1)S(1)}, bf16[128,4096]{1,0:T(8,128)(2,1)}, u32[]{:S(2)}, u32[]{:S(2)}) collective-permute-start(bf16[128,4096]{1,0:T(8,128)(2,1)S(1)} %maximum_select_fusion.refs_0_), channel_id=1, source_target_pairs={{0,2},{2,0},{4,6},{6,4},{8,10},{10,8},{12,14},{14,12},{16,18},{18,... | collective-permute-start | bytes 3145736 | tf_op jit(solution)/shard_map/ppermute | solution.py:125
  93.0 43.3 %collective-permute-start.23 = (bf16[128,4096]{1,0:T(8,128)(2,1)S(1)}, bf16[128,4096]{1,0:T(8,128)(2,1)}, u32[]{:S(2)}, u32[]{:S(2)}) collective-permute-start(bf16[128,4096]{1,0:T(8,128)(2,1)S(1)} %collective-permute-done.21.refs_4_), channel_id=1, source_target_pairs={{0,4},{2,6},{4,0},{6,2},{8,12},{10,14},{12,8},{14,10},{16,20},{18,... | collective-permute-start | bytes 3145736 | tf_op jit(solution)/shard_map/ppermute | solution.py:125
  96.1 41.9 %collective-permute-start.22 = (bf16[128,4096]{1,0:T(8,128)(2,1)S(1)}, bf16[128,4096]{1,0:T(8,128)(2,1)}, u32[]{:S(2)}, u32[]{:S(2)}) collective-permute-start(bf16[128,4096]{1,0:T(8,128)(2,1)S(1)} %collective-permute-done.21.refs_4_), channel_id=1, source_target_pairs={{0,2},{2,0},{4,6},{6,4},{8,10},{10,8},{12,14},{14,12},{16,18},{18,... | collective-permute-start | bytes 3145736 | tf_op jit(solution)/shard_map/ppermute | solution.py:125
  96.3 67.7 %collective-permute-start.37 = (bf16[128,4096]{1,0:T(8,128)(2,1)}, bf16[128,4096]{1,0:T(8,128)(2,1)}, u32[]{:S(2)}, u32[]{:S(2)}) collective-permute-start(bf16[128,4096]{1,0:T(8,128)(2,1)} %collective-permute-done.36), channel_id=1, source_target_pairs={{8,0},{10,2},{12,4},{14,6},{16,24},{18,26},{20,28},{22,30},{9,1},{... | collective-permute-start | bytes 3145736 | tf_op jit(solution)/shard_map/ppermute | solution.py:129
  98.7 79.7 %all-to-all-start.1 = ((bf16[256,16,128]{2,0,1:T(8,128)(2,1)}), bf16[256,16,128]{2,0,1:T(8,128)(2,1)}, u32[]{:S(2)}, u32[]{:S(2)}) async-start(bf16[256,16,128]{2,0,1:T(8,128)(2,1)} %copy_bitcast_fusion.1), calls=%async_computation.1 | async-start | bytes 2097152 | tf_op jit(solution)/shard_map/all_to_all | solution.py:372
  132.9 33.4 %collective-permute-start.20 = (bf16[128,4096]{1,0:T(8,128)(2,1)}, bf16[128,4096]{1,0:T(8,128)(2,1)S(1)}, u32[]{:S(2)}, u32[]{:S(2)}) collective-permute-start(bf16[128,4096]{1,0:T(8,128)(2,1)} %collective-permute-done.19.refs_2_), channel_id=1, source_target_pairs={{0,2},{2,0},{4,6},{6,4},{8,10},{10,8},{12,14},{14,12},{16,18},{18,... | collective-permute-start | bytes 3145736 | tf_op jit(solution)/shard_map/ppermute | solution.py:125
  134.7 39.5 %collective-permute-start.34 = (bf16[4096,128]{1,0:T(8,128)(2,1)S(1)}, bf16[4096,128]{1,0:T(8,128)(2,1)S(1)}, u32[]{:S(2)}, u32[]{:S(2)}) collective-permute-start(bf16[4096,128]{1,0:T(8,128)(2,1)S(1)} %bitcast.46), channel_id=1, source_target_pairs={{0,1},{1,0},{2,3},{3,2},{4,5},{5,4},{6,7},{7,6},{8,9},{9,8},{10,11... | collective-permute-start | bytes 3145736 | tf_op jit(solution)/shard_map/ppermute | solution.py:125
  136.3 33.5 %collective-permute-start.28 = (bf16[128,4096]{1,0:T(8,128)(2,1)S(1)}, bf16[128,4096]{1,0:T(8,128)(2,1)}, u32[]{:S(2)}, u32[]{:S(2)}) collective-permute-start(bf16[128,4096]{1,0:T(8,128)(2,1)S(1)} %broadcast_select_fusion.1.refs_8_), channel_id=1, source_target_pairs={{0,4},{2,6},{4,0},{6,2},{8,12},{10,14},{12,8},{14,10},{16,20},{18,... | collective-permute-start | bytes 3145736 | tf_op jit(solution)/shard_map/ppermute | solution.py:125
  138.0 37.9 %collective-permute-start.27 = (bf16[128,4096]{1,0:T(8,128)(2,1)S(1)}, bf16[128,4096]{1,0:T(8,128)(2,1)S(1)}, u32[]{:S(2)}, u32[]{:S(2)}) collective-permute-start(bf16[128,4096]{1,0:T(8,128)(2,1)S(1)} %broadcast_select_fusion.1.refs_8_), channel_id=1, source_target_pairs={{0,2},{2,0},{4,6},{6,4},{8,10},{10,8},{12,14},{14,12},{16,18},{18,... | collective-permute-start | bytes 3145736 | tf_op jit(solution)/shard_map/ppermute | solution.py:125
  174.2 39.6 %collective-permute-start.12 = (bf16[256,2048]{1,0:T(8,128)(2,1)}, bf16[256,2048]{1,0:T(8,128)(2,1)}, u32[]{:S(2)}, u32[]{:S(2)}) collective-permute-start(bf16[256,2048]{1,0:T(8,128)(2,1)} %collective-permute-done.3.refs_4_), channel_id=1, source_target_pairs={{8,16},{10,18},{12,20},{14,22},{16,8},{18,10},{20,12},{22,14},{9,1... | collective-permute-start | bytes 3145736 | tf_op jit(solution)/shard_map/ppermute | solution.py:129
  176.9 38.5 %collective-permute-start.30 = (bf16[4096,128]{1,0:T(8,128)(2,1)}, bf16[4096,128]{1,0:T(8,128)(2,1)}, u32[]{:S(2)}, u32[]{:S(2)}) collective-permute-start(bf16[4096,128]{1,0:T(8,128)(2,1)} %bitcast.5.refs_12_.refs_4_), channel_id=1, source_target_pairs={{0,1},{1,0},{2,3},{3,2},{4,5},{5,4},{6,7},{7,6},{8,9},{9,8},{10,11... | collective-permute-start | bytes 3145736 | tf_op jit(solution)/shard_map/ppermute | solution.py:125
  178.4 46.8 %collective-permute-start.31 = (bf16[4096,128]{1,0:T(8,128)(2,1)}, bf16[4096,128]{1,0:T(8,128)(2,1)}, u32[]{:S(2)}, u32[]{:S(2)}) collective-permute-start(bf16[4096,128]{1,0:T(8,128)(2,1)} %bitcast.7.refs_13_.refs_5_), channel_id=1, source_target_pairs={{0,1},{1,0},{2,3},{3,2},{4,5},{5,4},{6,7},{7,6},{8,9},{9,8},{10,11... | collective-permute-start | bytes 3145736 | tf_op jit(solution)/shard_map/ppermute | solution.py:125
  192.2 55.1 %collective-permute-start.38 = (bf16[128,4096]{1,0:T(8,128)(2,1)}, bf16[128,4096]{1,0:T(8,128)(2,1)}, u32[]{:S(2)}, u32[]{:S(2)}) collective-permute-start(bf16[128,4096]{1,0:T(8,128)(2,1)} %broadcast_select_fusion.refs_0_), channel_id=1, source_target_pairs={{0,2},{2,0},{4,6},{6,4},{8,10},{10,8},{12,14},{14,12},{16,18},{18,... | collective-permute-start | bytes 3145736 | tf_op jit(solution)/shard_map/ppermute | solution.py:125
  196.4 51.8 %collective-permute-start.40 = (bf16[128,4096]{1,0:T(8,128)(2,1)}, bf16[128,4096]{1,0:T(8,128)(2,1)}, u32[]{:S(2)}, u32[]{:S(2)}) collective-permute-start(bf16[128,4096]{1,0:T(8,128)(2,1)} %collective-permute-done.39.refs_2_), channel_id=1, source_target_pairs={{0,2},{2,0},{4,6},{6,4},{8,10},{10,8},{12,14},{14,12},{16,18},{18,... | collective-permute-start | bytes 3145736 | tf_op jit(solution)/shard_map/ppermute | solution.py:125
  213.8 86.2 %collective-permute-start.1 = (bf16[256,2048]{1,0:T(8,128)(2,1)}, bf16[256,2048]{1,0:T(8,128)(2,1)}, u32[]{:S(2)}, u32[]{:S(2)}) collective-permute-start(bf16[256,2048]{1,0:T(8,128)(2,1)} %refs_0_.1), channel_id=1, source_target_pairs={{0,4},{2,6},{4,0},{6,2},{8,12},{10,14},{12,8},{14,10},{16,20},{18,... | collective-permute-start | bytes 3145736 | tf_op jit(solution)/shard_map/ppermute | solution.py:125
  215.4 85.1 %collective-permute-start.8 = (bf16[256,2048]{1,0:T(8,128)(2,1)}, bf16[256,2048]{1,0:T(8,128)(2,1)}, u32[]{:S(2)}, u32[]{:S(2)}) collective-permute-start(bf16[256,2048]{1,0:T(8,128)(2,1)} %collective-permute-done.7), channel_id=1, source_target_pairs={{8,0},{10,2},{12,4},{14,6},{16,24},{18,26},{20,28},{22,30},{9,1},{... | collective-permute-start | bytes 3145736 | tf_op jit(solution)/shard_map/ppermute | solution.py:129
  225.2 38.1 %collective-permute-start.35 = (bf16[1536,128]{1,0:T(8,128)(2,1)}, bf16[1536,128]{1,0:T(8,128)(2,1)}, u32[]{:S(2)}, u32[]{:S(2)}) collective-permute-start(bf16[1536,128]{1,0:T(8,128)(2,1)} %get-tuple-element.26), channel_id=1, source_target_pairs={{0,1},{1,0},{2,3},{3,2},{4,5},{5,4},{6,7},{7,6},{8,9},{9,8},{10,11... | collective-permute-start | bytes 1179656 | tf_op jit(solution)/shard_map/ppermute | solution.py:125
  248.3 53.7 %collective-permute-start.13 = (bf16[256,2048]{1,0:T(8,128)(2,1)}, bf16[256,2048]{1,0:T(8,128)(2,1)}, u32[]{:S(2)}, u32[]{:S(2)}) collective-permute-start(bf16[256,2048]{1,0:T(8,128)(2,1)} %collective-permute-done.12), channel_id=1, source_target_pairs={{8,0},{10,2},{12,4},{14,6},{16,24},{18,26},{20,28},{22,30},{9,1},{... | collective-permute-start | bytes 3145736 | tf_op jit(solution)/shard_map/ppermute | solution.py:129
  267.3 38.0 %collective-permute-start = (bf16[256,2048]{1,0:T(8,128)(2,1)}, bf16[256,2048]{1,0:T(8,128)(2,1)S(1)}, u32[]{:S(2)}, u32[]{:S(2)}) collective-permute-start(bf16[256,2048]{1,0:T(8,128)(2,1)} %refs_0_.1), channel_id=1, source_target_pairs={{0,2},{2,0},{4,6},{6,4},{8,10},{10,8},{12,14},{14,12},{16,18},{18,... | collective-permute-start | bytes 3145736 | tf_op jit(solution)/shard_map/ppermute | solution.py:125
  274.9 31.5 %collective-permute-start.5 = (bf16[256,2048]{1,0:T(8,128)(2,1)}, bf16[256,2048]{1,0:T(8,128)(2,1)}, u32[]{:S(2)}, u32[]{:S(2)}) collective-permute-start(bf16[256,2048]{1,0:T(8,128)(2,1)} %collective-permute-done.3.refs_4_), channel_id=1, source_target_pairs={{0,4},{2,6},{4,0},{6,2},{8,12},{10,14},{12,8},{14,10},{16,20},{18,... | collective-permute-start | bytes 3145736 | tf_op jit(solution)/shard_map/ppermute | solution.py:125
  292.6 67.8 %all-to-all-start.3 = ((bf16[16,256,128]{2,1,0:T(8,128)(2,1)}), bf16[16,256,128]{2,1,0:T(8,128)(2,1)}, u32[]{:S(2)}, u32[]{:S(2)}) async-start(bf16[16,256,128]{2,1,0:T(8,128)(2,1)} %bitcast.20), calls=%async_computation.3 | async-start | bytes 2097152 | tf_op jit(solution)/shard_map/all_to_all | solution.py:416
  302.0 35.5 %collective-permute-start.10 = (bf16[256,2048]{1,0:T(8,128)(2,1)S(1)}, bf16[256,2048]{1,0:T(8,128)(2,1)}, u32[]{:S(2)}, u32[]{:S(2)}) collective-permute-start(bf16[256,2048]{1,0:T(8,128)(2,1)S(1)} %broadcast_select_fusion.3.refs_8_), channel_id=1, source_target_pairs={{0,4},{2,6},{4,0},{6,2},{8,12},{10,14},{12,8},{14,10},{16,20},{18,... | collective-permute-start | bytes 3145736 | tf_op jit(solution)/shard_map/ppermute | solution.py:125
  306.3 53.1 %collective-permute-start.15 = (bf16[256,2048]{1,0:T(8,128)(2,1)S(1)}, bf16[256,2048]{1,0:T(8,128)(2,1)}, u32[]{:S(2)}, u32[]{:S(2)}) collective-permute-start(bf16[256,2048]{1,0:T(8,128)(2,1)S(1)} %broadcast_select_fusion.2.refs_12_), channel_id=1, source_target_pairs={{0,4},{2,6},{4,0},{6,2},{8,12},{10,14},{12,8},{14,10},{16,20},{18,... | collective-permute-start | bytes 3145736 | tf_op jit(solution)/shard_map/ppermute | solution.py:125
  306.4 53.0 %collective-permute-start.9 = (bf16[256,2048]{1,0:T(8,128)(2,1)S(1)}, bf16[256,2048]{1,0:T(8,128)(2,1)S(1)}, u32[]{:S(2)}, u32[]{:S(2)}) collective-permute-start(bf16[256,2048]{1,0:T(8,128)(2,1)S(1)} %broadcast_select_fusion.3.refs_8_), channel_id=1, source_target_pairs={{0,2},{2,0},{4,6},{6,4},{8,10},{10,8},{12,14},{14,12},{16,18},{18,... | collective-permute-start | bytes 3145736 | tf_op jit(solution)/shard_map/ppermute | solution.py:125
  307.4 53.7 %collective-permute-start.6 = (bf16[256,2048]{1,0:T(8,128)(2,1)}, bf16[256,2048]{1,0:T(8,128)(2,1)S(1)}, u32[]{:S(2)}, u32[]{:S(2)}) collective-permute-start(bf16[256,2048]{1,0:T(8,128)(2,1)} %collective-permute-done.5.refs_6_), channel_id=1, source_target_pairs={{0,2},{2,0},{4,6},{6,4},{8,10},{10,8},{12,14},{14,12},{16,18},{18,... | collective-permute-start | bytes 3145736 | tf_op jit(solution)/shard_map/ppermute | solution.py:125
  308.9 53.3 %collective-permute-start.14 = (bf16[256,2048]{1,0:T(8,128)(2,1)S(1)}, bf16[256,2048]{1,0:T(8,128)(2,1)}, u32[]{:S(2)}, u32[]{:S(2)}) collective-permute-start(bf16[256,2048]{1,0:T(8,128)(2,1)S(1)} %broadcast_select_fusion.2.refs_12_), channel_id=1, source_target_pairs={{0,2},{2,0},{4,6},{6,4},{8,10},{10,8},{12,14},{14,12},{16,18},{18,... | collective-permute-start | bytes 3145736 | tf_op jit(solution)/shard_map/ppermute | solution.py:125
  (61 other events, 637.1 us)
